TPU v7x, 8 devices: a whole 2x2x1 slice. The times are simulated.
8 devices in a mesh: dp: 2 (over z, y), cp: 4 (over x, core).
Axes of the slice: x: 2, y: 2, z: 1, core: 2. Of those that a mesh axis runs over, the one named last changes fastest.
Arguments:
- q_tok: bfloat16 [4096, 6, 128], P(('dp', 'cp')), parts along dimension 0
- k_tok: bfloat16 [4096, 128], P(('dp', 'cp')), parts along dimension 0
- v_tok: bfloat16 [4096, 128], P(('dp', 'cp')), parts along dimension 0
- fwd_out: bfloat16 [4096, 6, 128], P(('dp', 'cp')), parts along dimension 0
- d_out: bfloat16 [4096, 6, 128], P(('dp', 'cp')), parts along dimension 0
- lse_row: float32 [4096, 6], P(('dp', 'cp')), parts along dimension 0
Outputs:
- output 1: bfloat16 [4096, 6, 128], P(('dp', 'cp')), parts along dimension 0
- output 2: bfloat16 [4096, 128], P(('dp', 'cp')), parts along dimension 0
- output 3: bfloat16 [4096, 128], P(('dp', 'cp')), parts along dimension 0
There are 2 independent parts. A program takes and returns all parts, laid end to end along the dimension named above; each array names one.
All inputs are finite; a program needn't handle non-finite values.
Results may differ from a plain program's by a relative error of at most 0.001.
Values are sent between devices in bfloat16 or wider.
A program may use at most 1 GiB of HBM per device.

v0:
```python
import jax
import jax.numpy as jnp
from jax import lax
from jax.sharding import PartitionSpec as P


def pair_scores(q_block, do_block, lse_block, delta_block, k_block, v_block, on_diag, softmax_scale):
    logits = jnp.einsum('rgd,cd->rgc', q_block, k_block, preferred_element_type=jnp.float32)
    row_ids = jnp.arange(q_block.shape[0])
    allowed = jnp.logical_or(row_ids[None, :] <= row_ids[:, None], jnp.logical_not(on_diag))
    prob_mat = jnp.exp(jnp.where(allowed[:, None, :], logits * softmax_scale - lse_block[:, :, None], -jnp.inf))
    d_prob = jnp.einsum('rgd,cd->rgc', do_block, v_block, preferred_element_type=jnp.float32)
    d_score = (prob_mat * (d_prob - delta_block[:, :, None])).astype(jnp.bfloat16)
    return prob_mat.astype(jnp.bfloat16), d_score


def solution(mesh):
    n_dev = mesh.shape['cp']
    forward_perm = [(i, (i + 1) % n_dev) for i in range(n_dev)]
    row_spec = P(('dp', 'cp'))

    def local_fn(q_tok, k_tok, v_tok, fwd_out, d_out, lse_row):
        softmax_scale = q_tok.shape[-1] ** -0.5
        my_index = lax.axis_index('cp')
        row_delta = jnp.einsum('rgd,rgd->rg', d_out, fwd_out, preferred_element_type=jnp.float32)

        def accumulate(step, state):
            def pair_update(state_in):
                dq_acc, k_cur, v_cur, dk_acc, dv_acc = state_in
                prob_low, score_low = pair_scores(q_tok, d_out, lse_row, row_delta, k_cur, v_cur, step == 0, softmax_scale)
                dq_acc = dq_acc + jnp.einsum('rgc,cd->rgd', score_low, k_cur, preferred_element_type=jnp.float32)
                dk_acc = dk_acc + jnp.einsum('rgc,rgd->cd', score_low, q_tok, preferred_element_type=jnp.float32)
                dv_acc = dv_acc + jnp.einsum('rgc,rgd->cd', prob_low, d_out, preferred_element_type=jnp.float32)
                return (dq_acc, k_cur, v_cur, dk_acc, dv_acc)

            def keep_state(state_in):
                return state_in

            return lax.cond(step <= my_index, pair_update, keep_state, state)

        def step_fn(step, state):
            dq_acc, k_cur, v_cur, dk_acc, dv_acc = accumulate(step, state)
            k_next = lax.ppermute(k_cur, 'cp', forward_perm)
            v_next = lax.ppermute(v_cur, 'cp', forward_perm)
            dk_next = lax.ppermute(dk_acc, 'cp', forward_perm)
            dv_next = lax.ppermute(dv_acc, 'cp', forward_perm)
            return (dq_acc, k_next, v_next, dk_next, dv_next)

        kv_zeros = jnp.zeros(k_tok.shape, jnp.float32)
        state = (jnp.zeros(q_tok.shape, jnp.float32), k_tok, v_tok, kv_zeros, kv_zeros)
        state = lax.fori_loop(0, n_dev - 1, step_fn, state)
        dq_acc, k_cur, v_cur, dk_acc, dv_acc = accumulate(n_dev - 1, state)
        dk_home = lax.ppermute(dk_acc, 'cp', forward_perm)
        dv_home = lax.ppermute(dv_acc, 'cp', forward_perm)
        grad_q = (dq_acc * softmax_scale).astype(jnp.bfloat16)
        grad_k = (dk_home * softmax_scale).astype(jnp.bfloat16)
        grad_v = dv_home.astype(jnp.bfloat16)
        return grad_q, grad_k, grad_v

    return jax.shard_map(local_fn, mesh=mesh, in_specs=(row_spec, row_spec, row_spec, row_spec, row_spec, row_spec), out_specs=(row_spec, row_spec, row_spec), check_vma=False)
```

profile of v0, /device:TPU:0, one launch (start us, length us, event | category | flops | bytes accessed | tf_op | source)
XLA Modules:
  0.0 82.1 jit_solution(9429061485542745348)
XLA Ops:
  0.6 0.9 %copy.56 = bf16[512,128]{1,0:T(8,128)(2,1)S(1)} copy(bf16[512,128]{1,0:T(8,128)(2,1)} %param.13) | data formatting | bytes 262144
  1.5 1.6 %copy.57 = bf16[512,128]{1,0:T(8,128)(2,1)} copy(bf16[512,128]{1,0:T(8,128)(2,1)} %param.14) | data formatting | bytes 262144
  3.1 1.8 %fusion.35 = f32[512,6]{0,1:T(8,128)S(1)} fusion(bf16[512,6,128]{2,0,1:T(8,128)(2,1)} %param.16, bf16[512,6,128]{2,0,1:T(8,128)(2,1)} %param.15), kind=kLoop, calls=%fused_computation.35 | loop fusion | flops 1569792 | bytes 1585152 | tf_op jit(solution)/shard_map/rgd,rgd->rg/dot_general | solution.py:25
  5.1 61.8 %while.21 = (s32[]{:T(128)}, f32[512,6,128]{2,0,1:T(8,128)S(1)}, bf16[512,128]{1,0:T(8,128)(2,1)S(1)}, bf16[512,128]{1,0:T(8,128)(2,1)}, f32[512,128]{1,0:T(8,12...) while((s32[]{:T(128)}, f32[512,6,128]{2,0,1:T(8,128)S(1)}, ...), condition=%wide.region_3.4_spmd, body=%wide.region_0.3_spmd.sunk | while | flops 2030043136 | bytes 47927816 | solution.py:51
  5.1 0.9 %copy.37 = bf16[512,128]{1,0:T(8,128)(2,1)S(1)} copy(bf16[512,128]{1,0:T(8,128)(2,1)} %get-tuple-element.392) | data formatting | bytes 262144 | tf_op jit(solution)/shard_map
  6.1 8.9 %conditional.4 = ((f32[512,6,128]{2,0,1:T(8,128)S(1)}, f32[512,128]{1,0:T(8,128)S(1)}, f32[512,128]{1,0:T(8,128)S(1)})) conditional(s32[]{:T(128)} %convert_element_type.52, (f32[512,6,128]{2,0,1:T(8,128)S(1)}, f32[512,128]{1,0:T(8,128)S(1)}, f32[512,128]{1,0:T(8,128)S(1)}) %tuple.50, (s32[]{:T(128)}, bf16[512,6,128]{2,0,1:T(8,128)(2,1)}, ...), branch_computations={%region_1.0_spmd, %region_2.2_spmd} | conditional | flops 2030043136 | bytes 43208832 | solution.py:39
  6.2 2.2 %fusion.14 = f32[512,6,512]{2,0,1:T(8,128)S(1)} fusion(bf16[512,6,128]{2,0,1:T(8,128)(2,1)} %get-tuple-element.225, bf16[512,128]{1,0:T(8,128)(2,1)S(1)} %get-tuple-element.226), kind=kOutput, calls=%fused_computation.14 | convolution fusion | flops 402653184 | bytes 7208960 | tf_op jit(solution)/shard_map/while/body/eval_jaxpr/cond/branch_1_fun/rgd,cd->rgc/dot_general | solution.py:8
  8.4 2.0 %fusion.7 = f32[512,128]{1,0:T(8,128)S(1)} fusion(f32[512,128]{1,0:T(8,128)S(1)} %get-tuple-element.232, bf16[512,6,128]{2,0,1:T(8,128)(2,1)S(1)} %copy-done.2, f32[512,6,512]{2,0,1:T(8,128)S(1)} %fusion.14, f32[512,6]{0,1:T(8,128)S(1)} %copy-done.4, pred[512,512]{1,0:T(8,128)(4,1)S(1)} %fusion.11), kind=kOutput, calls=%fused_computation.8 | convolution fusion | flops 409010176 | bytes 7876608 | tf_op jit(solution)/shard_map/while/body/eval_jaxpr/cond/branch_1_fun/rgc,rgd->cd/dot_general | solution.py:33
  10.5 2.5 %multiply_convert_fusion = bf16[512,6,512]{2,0,1:T(8,128)(2,1)S(1)} fusion(f32[512,6,512]{2,0,1:T(8,128)S(1)} %fusion.14, f32[512,6]{0,1:T(8,128)S(1)} %get-tuple-element.230, f32[512,6]{0,1:T(8,128)S(1)} %copy-done.4, pred[512,512]{1,0:T(8,128)(4,1)S(1)} %fusion.11, bf16[512,6,128]{2,0,1:T(8,128)(2,1)S(1)} %copy-done.2, ...), kind=kOutput, calls=%fused_computation | convolution fusion | flops 412090368 | bytes 10641408 | tf_op jit(solution)/shard_map/while/body/eval_jaxpr/cond/branch_1_fun/rgd,cd->rgc/dot_general | solution.py:12
  12.9 1.0 %fusion.10 = f32[512,128]{1,0:T(8,128)S(1)} fusion(f32[512,128]{1,0:T(8,128)S(1)} %get-tuple-element.231, bf16[512,6,512]{2,0,1:T(8,128)(2,1)S(1)} %multiply_convert_fusion, bf16[512,6,128]{2,0,1:T(8,128)(2,1)S(1)} %copy-done), kind=kOutput, calls=%fused_computation.9 | convolution fusion | flops 402718720 | bytes 4456448 | tf_op jit(solution)/shard_map/while/body/eval_jaxpr/cond/branch_1_fun/rgc,rgd->cd/dot_general | solution.py:32
  14.0 1.0 %convolution_add_fusion = f32[512,6,128]{2,0,1:T(8,128)S(1)} fusion(f32[512,6,128]{2,0,1:T(8,128)S(1)} %get-tuple-element.223, bf16[512,6,512]{2,0,1:T(8,128)(2,1)S(1)} %multiply_convert_fusion, bf16[512,128]{1,0:T(8,128)(2,1)S(1)} %get-tuple-element.226), kind=kOutput, calls=%fused_computation.5 | convolution fusion | flops 403046400 | bytes 6422528 | tf_op jit(solution)/shard_map/while/body/eval_jaxpr/cond/branch_1_fun/rgc,cd->rgd/dot_general | solution.py:31
  15.9 2.6 %collective-permute-start.3 = (f32[512,128]{1,0:T(8,128)S(1)}, f32[512,128]{1,0:T(8,128)S(1)}, u32[]{:S(2)}, u32[]{:S(2)}) collective-permute-start(f32[512,128]{1,0:T(8,128)S(1)} %get-tuple-element.370), channel_id=1, source_target_pairs={{0,1},{1,2},{2,3},{3,0},{4,5},{5,6},{6,7},{7,4}} | collective-permute-start | bytes 786440 | tf_op jit(solution)/shard_map/while/body/eval_jaxpr/ppermute | solution.py:46
  18.6 3.3 %collective-permute-done.2 = f32[512,128]{1,0:T(8,128)S(1)} collective-permute-done((f32[512,128]{1,0:T(8,128)S(1)}, f32[512,128]{1,0:T(8,128)S(1)}, u32[]{:S(2)}, u32[]{:S(2)}) %collective-permute-start.2) | collective-permute-done | bytes 262176 | tf_op jit(solution)/shard_map/while/body/eval_jaxpr/ppermute | solution.py:45
  21.9 2.8 %collective-permute-done.3 = f32[512,128]{1,0:T(8,128)S(1)} collective-permute-done((f32[512,128]{1,0:T(8,128)S(1)}, f32[512,128]{1,0:T(8,128)S(1)}, u32[]{:S(2)}, u32[]{:S(2)}) %collective-permute-start.3) | collective-permute-done | bytes 262176 | tf_op jit(solution)/shard_map/while/body/eval_jaxpr/ppermute | solution.py:46
  24.7 1.4 %collective-permute-done = bf16[512,128]{1,0:T(8,128)(2,1)S(1)} collective-permute-done((bf16[512,128]{1,0:T(8,128)(2,1)S(1)}, bf16[512,128]{1,0:T(8,128)(2,1)S(1)}, u32[]{:S(2)}, u32[]{:S(2)}) %collective-permute-start) | collective-permute-done | bytes 131104 | tf_op jit(solution)/shard_map/while/body/eval_jaxpr/ppermute | solution.py:43
  26.1 1.4 %collective-permute-done.1 = bf16[512,128]{1,0:T(8,128)(2,1)} collective-permute-done((bf16[512,128]{1,0:T(8,128)(2,1)S(1)}, bf16[512,128]{1,0:T(8,128)(2,1)}, u32[]{:S(2)}, u32[]{:S(2)}) %collective-permute-start.1) | collective-permute-done | bytes 131104 | tf_op jit(solution)/shard_map/while/body/eval_jaxpr/ppermute | solution.py:44
  27.5 0.9 %copy.37 = bf16[512,128]{1,0:T(8,128)(2,1)S(1)} copy(bf16[512,128]{1,0:T(8,128)(2,1)} %get-tuple-element.392) | data formatting | bytes 262144 | tf_op jit(solution)/shard_map
  28.4 8.9 %collective-permute-start.2 = (f32[512,128]{1,0:T(8,128)S(1)}, f32[512,128]{1,0:T(8,128)S(1)}, u32[]{:S(2)}, u32[]{:S(2)}) collective-permute-start(f32[512,128]{1,0:T(8,128)S(1)} %get-tuple-element.369), channel_id=1, source_target_pairs={{0,1},{1,2},{2,3},{3,0},{4,5},{5,6},{6,7},{7,4}} | collective-permute-start | bytes 786440 | tf_op jit(solution)/shard_map/while/body/eval_jaxpr/ppermute | solution.py:45
  37.3 2.5 %collective-permute-start.3 = (f32[512,128]{1,0:T(8,128)S(1)}, f32[512,128]{1,0:T(8,128)S(1)}, u32[]{:S(2)}, u32[]{:S(2)}) collective-permute-start(f32[512,128]{1,0:T(8,128)S(1)} %get-tuple-element.370), channel_id=1, source_target_pairs={{0,1},{1,2},{2,3},{3,0},{4,5},{5,6},{6,7},{7,4}} | collective-permute-start | bytes 786440 | tf_op jit(solution)/shard_map/while/body/eval_jaxpr/ppermute | solution.py:46
  40.7 2.8 %collective-permute-done.3 = f32[512,128]{1,0:T(8,128)S(1)} collective-permute-done((f32[512,128]{1,0:T(8,128)S(1)}, f32[512,128]{1,0:T(8,128)S(1)}, u32[]{:S(2)}, u32[]{:S(2)}) %collective-permute-start.3) | collective-permute-done | bytes 262176 | tf_op jit(solution)/shard_map/while/body/eval_jaxpr/ppermute | solution.py:46
  43.5 1.4 %collective-permute-done = bf16[512,128]{1,0:T(8,128)(2,1)S(1)} collective-permute-done((bf16[512,128]{1,0:T(8,128)(2,1)S(1)}, bf16[512,128]{1,0:T(8,128)(2,1)S(1)}, u32[]{:S(2)}, u32[]{:S(2)}) %collective-permute-start) | collective-permute-done | bytes 131104 | tf_op jit(solution)/shard_map/while/body/eval_jaxpr/ppermute | solution.py:43
  44.9 1.4 %collective-permute-done.1 = bf16[512,128]{1,0:T(8,128)(2,1)} collective-permute-done((bf16[512,128]{1,0:T(8,128)(2,1)S(1)}, bf16[512,128]{1,0:T(8,128)(2,1)}, u32[]{:S(2)}, u32[]{:S(2)}) %collective-permute-start.1) | collective-permute-done | bytes 131104 | tf_op jit(solution)/shard_map/while/body/eval_jaxpr/ppermute | solution.py:44
  47.2 2.4 %collective-permute-start.2 = (f32[512,128]{1,0:T(8,128)S(1)}, f32[512,128]{1,0:T(8,128)S(1)}, u32[]{:S(2)}, u32[]{:S(2)}) collective-permute-start(f32[512,128]{1,0:T(8,128)S(1)} %get-tuple-element.369), channel_id=1, source_target_pairs={{0,1},{1,2},{2,3},{3,0},{4,5},{5,6},{6,7},{7,4}} | collective-permute-start | bytes 786440 | tf_op jit(solution)/shard_map/while/body/eval_jaxpr/ppermute | solution.py:45
  49.7 11.4 %collective-permute-start.3 = (f32[512,128]{1,0:T(8,128)S(1)}, f32[512,128]{1,0:T(8,128)S(1)}, u32[]{:S(2)}, u32[]{:S(2)}) collective-permute-start(f32[512,128]{1,0:T(8,128)S(1)} %get-tuple-element.370), channel_id=1, source_target_pairs={{0,1},{1,2},{2,3},{3,0},{4,5},{5,6},{6,7},{7,4}} | collective-permute-start | bytes 786440 | tf_op jit(solution)/shard_map/while/body/eval_jaxpr/ppermute | solution.py:46
  61.2 1.1 %collective-permute-done.3 = f32[512,128]{1,0:T(8,128)S(1)} collective-permute-done((f32[512,128]{1,0:T(8,128)S(1)}, f32[512,128]{1,0:T(8,128)S(1)}, u32[]{:S(2)}, u32[]{:S(2)}) %collective-permute-start.3) | collective-permute-done | bytes 262176 | tf_op jit(solution)/shard_map/while/body/eval_jaxpr/ppermute | solution.py:46
  62.3 3.2 %collective-permute-done = bf16[512,128]{1,0:T(8,128)(2,1)S(1)} collective-permute-done((bf16[512,128]{1,0:T(8,128)(2,1)S(1)}, bf16[512,128]{1,0:T(8,128)(2,1)S(1)}, u32[]{:S(2)}, u32[]{:S(2)}) %collective-permute-start) | collective-permute-done | bytes 131104 | tf_op jit(solution)/shard_map/while/body/eval_jaxpr/ppermute | solution.py:43
  65.5 1.4 %collective-permute-done.1 = bf16[512,128]{1,0:T(8,128)(2,1)} collective-permute-done((bf16[512,128]{1,0:T(8,128)(2,1)S(1)}, bf16[512,128]{1,0:T(8,128)(2,1)}, u32[]{:S(2)}, u32[]{:S(2)}) %collective-permute-start.1) | collective-permute-done | bytes 131104 | tf_op jit(solution)/shard_map/while/body/eval_jaxpr/ppermute | solution.py:44
  66.9 3.1 %collective-permute-start.5 = (bf16[512,128]{1,0:T(8,128)(2,1)S(1)}, bf16[512,128]{1,0:T(8,128)(2,1)S(1)}, u32[]{:S(2)}, u32[]{:S(2)}) collective-permute-start(bf16[512,128]{1,0:T(8,128)(2,1)S(1)} %convert.12), channel_id=1, source_target_pairs={{0,1},{1,2},{2,3},{3,0},{4,5},{5,6},{6,7},{7,4}} | collective-permute-start | bytes 393224 | tf_op jit(solution)/shard_map/ppermute | solution.py:54
  70.1 2.5 %collective-permute-start.4 = (f32[512,128]{1,0:T(8,128)S(1)}, f32[512,128]{1,0:T(8,128)S(1)}, u32[]{:S(2)}, u32[]{:S(2)}) collective-permute-start(f32[512,128]{1,0:T(8,128)S(1)} %get-tuple-element.274), channel_id=1, source_target_pairs={{0,1},{1,2},{2,3},{3,0},{4,5},{5,6},{6,7},{7,4}} | collective-permute-start | bytes 786440 | tf_op jit(solution)/shard_map/ppermute | solution.py:53
  72.6 1.0 %multiply_convert_fusion.2 = bf16[512,6,128]{2,0,1:T(8,128)(2,1)} fusion(f32[512,6,128]{2,0,1:T(8,128)S(1)} %get-tuple-element.273), kind=kLoop, calls=%fused_computation.36 | loop fusion | flops 786432 | bytes 2359296 | tf_op jit(solution)/shard_map/convert_element_type | solution.py:55
  73.6 4.4 %collective-permute-done.5 = bf16[512,128]{1,0:T(8,128)(2,1)S(1)} collective-permute-done((bf16[512,128]{1,0:T(8,128)(2,1)S(1)}, bf16[512,128]{1,0:T(8,128)(2,1)S(1)}, u32[]{:S(2)}, u32[]{:S(2)}) %collective-permute-start.5) | collective-permute-done | bytes 131104 | tf_op jit(solution)/shard_map/ppermute | solution.py:54
  78.0 2.8 %collective-permute-done.4 = f32[512,128]{1,0:T(8,128)S(1)} collective-permute-done((f32[512,128]{1,0:T(8,128)S(1)}, f32[512,128]{1,0:T(8,128)S(1)}, u32[]{:S(2)}, u32[]{:S(2)}) %collective-permute-start.4) | collective-permute-done | bytes 262176 | tf_op jit(solution)/shard_map/ppermute | solution.py:53
  (35 shorter events, 4.6 us)
Async XLA Ops:
  6.1 2.3 %copy-start.2 = (bf16[512,6,128]{2,0,1:T(8,128)(2,1)S(1)}, bf16[512,6,128]{2,0,1:T(8,128)(2,1)}, u32[]{:S(2)}) copy-start(bf16[512,6,128]{2,0,1:T(8,128)(2,1)} %get-tuple-element.228) | copy-start | bytes 2359300 | tf_op jit(solution)/shard_map/while/body/eval_jaxpr/cond
  6.1 2.3 %copy-start.4 = (f32[512,6]{0,1:T(8,128)S(1)}, f32[512,6]{0,1:T(8,128)}, u32[]{:S(2)}) copy-start(f32[512,6]{0,1:T(8,128)} %get-tuple-element.227) | copy-start | bytes 36868 | tf_op jit(solution)/shard_map/while/body/eval_jaxpr/cond
  10.4 2.5 %copy-start = (bf16[512,6,128]{2,0,1:T(8,128)(2,1)S(1)}, bf16[512,6,128]{2,0,1:T(8,128)(2,1)}, u32[]{:S(2)}) copy-start(bf16[512,6,128]{2,0,1:T(8,128)(2,1)} %get-tuple-element.225) | copy-start | bytes 2359300 | tf_op jit(solution)/shard_map/while/body/eval_jaxpr/cond
  15.0 6.9 %collective-permute-start.2 = (f32[512,128]{1,0:T(8,128)S(1)}, f32[512,128]{1,0:T(8,128)S(1)}, u32[]{:S(2)}, u32[]{:S(2)}) collective-permute-start(f32[512,128]{1,0:T(8,128)S(1)} %get-tuple-element.369), channel_id=1, source_target_pairs={{0,1},{1,2},{2,3},{3,0},{4,5},{5,6},{6,7},{7,4}} | collective-permute-start | bytes 786440 | tf_op jit(solution)/shard_map/while/body/eval_jaxpr/ppermute | solution.py:45
  15.9 8.8 %collective-permute-start.3 = (f32[512,128]{1,0:T(8,128)S(1)}, f32[512,128]{1,0:T(8,128)S(1)}, u32[]{:S(2)}, u32[]{:S(2)}) collective-permute-start(f32[512,128]{1,0:T(8,128)S(1)} %get-tuple-element.370), channel_id=1, source_target_pairs={{0,1},{1,2},{2,3},{3,0},{4,5},{5,6},{6,7},{7,4}} | collective-permute-start | bytes 786440 | tf_op jit(solution)/shard_map/while/body/eval_jaxpr/ppermute | solution.py:46
  18.5 7.6 %collective-permute-start = (bf16[512,128]{1,0:T(8,128)(2,1)S(1)}, bf16[512,128]{1,0:T(8,128)(2,1)S(1)}, u32[]{:S(2)}, u32[]{:S(2)}) collective-permute-start(bf16[512,128]{1,0:T(8,128)(2,1)S(1)} %copy.36), channel_id=1, source_target_pairs={{0,1},{1,2},{2,3},{3,0},{4,5},{5,6},{6,7},{7,4}} | collective-permute-start | bytes 393224 | tf_op jit(solution)/shard_map/while/body/eval_jaxpr/ppermute | solution.py:43
  18.5 9.0 %collective-permute-start.1 = (bf16[512,128]{1,0:T(8,128)(2,1)S(1)}, bf16[512,128]{1,0:T(8,128)(2,1)}, u32[]{:S(2)}, u32[]{:S(2)}) collective-permute-start(bf16[512,128]{1,0:T(8,128)(2,1)S(1)} %copy.37), channel_id=1, source_target_pairs={{0,1},{1,2},{2,3},{3,0},{4,5},{5,6},{6,7},{7,4}} | collective-permute-start | bytes 393224 | tf_op jit(solution)/shard_map/while/body/eval_jaxpr/ppermute | solution.py:44
  28.4 12.3 %collective-permute-start.2 = (f32[512,128]{1,0:T(8,128)S(1)}, f32[512,128]{1,0:T(8,128)S(1)}, u32[]{:S(2)}, u32[]{:S(2)}) collective-permute-start(f32[512,128]{1,0:T(8,128)S(1)} %get-tuple-element.369), channel_id=1, source_target_pairs={{0,1},{1,2},{2,3},{3,0},{4,5},{5,6},{6,7},{7,4}} | collective-permute-start | bytes 786440 | tf_op jit(solution)/shard_map/while/body/eval_jaxpr/ppermute | solution.py:45
  37.3 6.2 %collective-permute-start.3 = (f32[512,128]{1,0:T(8,128)S(1)}, f32[512,128]{1,0:T(8,128)S(1)}, u32[]{:S(2)}, u32[]{:S(2)}) collective-permute-start(f32[512,128]{1,0:T(8,128)S(1)} %get-tuple-element.370), channel_id=1, source_target_pairs={{0,1},{1,2},{2,3},{3,0},{4,5},{5,6},{6,7},{7,4}} | collective-permute-start | bytes 786440 | tf_op jit(solution)/shard_map/while/body/eval_jaxpr/ppermute | solution.py:46
  39.8 5.1 %collective-permute-start = (bf16[512,128]{1,0:T(8,128)(2,1)S(1)}, bf16[512,128]{1,0:T(8,128)(2,1)S(1)}, u32[]{:S(2)}, u32[]{:S(2)}) collective-permute-start(bf16[512,128]{1,0:T(8,128)(2,1)S(1)} %copy.36), channel_id=1, source_target_pairs={{0,1},{1,2},{2,3},{3,0},{4,5},{5,6},{6,7},{7,4}} | collective-permute-start | bytes 393224 | tf_op jit(solution)/shard_map/while/body/eval_jaxpr/ppermute | solution.py:43
  39.8 6.5 %collective-permute-start.1 = (bf16[512,128]{1,0:T(8,128)(2,1)S(1)}, bf16[512,128]{1,0:T(8,128)(2,1)}, u32[]{:S(2)}, u32[]{:S(2)}) collective-permute-start(bf16[512,128]{1,0:T(8,128)(2,1)S(1)} %copy.37), channel_id=1, source_target_pairs={{0,1},{1,2},{2,3},{3,0},{4,5},{5,6},{6,7},{7,4}} | collective-permute-start | bytes 393224 | tf_op jit(solution)/shard_map/while/body/eval_jaxpr/ppermute | solution.py:44
  47.2 13.9 %collective-permute-start.2 = (f32[512,128]{1,0:T(8,128)S(1)}, f32[512,128]{1,0:T(8,128)S(1)}, u32[]{:S(2)}, u32[]{:S(2)}) collective-permute-start(f32[512,128]{1,0:T(8,128)S(1)} %get-tuple-element.369), channel_id=1, source_target_pairs={{0,1},{1,2},{2,3},{3,0},{4,5},{5,6},{6,7},{7,4}} | collective-permute-start | bytes 786440 | tf_op jit(solution)/shard_map/while/body/eval_jaxpr/ppermute | solution.py:45
  49.7 12.6 %collective-permute-start.3 = (f32[512,128]{1,0:T(8,128)S(1)}, f32[512,128]{1,0:T(8,128)S(1)}, u32[]{:S(2)}, u32[]{:S(2)}) collective-permute-start(f32[512,128]{1,0:T(8,128)S(1)} %get-tuple-element.370), channel_id=1, source_target_pairs={{0,1},{1,2},{2,3},{3,0},{4,5},{5,6},{6,7},{7,4}} | collective-permute-start | bytes 786440 | tf_op jit(solution)/shard_map/while/body/eval_jaxpr/ppermute | solution.py:46
  61.1 4.4 %collective-permute-start = (bf16[512,128]{1,0:T(8,128)(2,1)S(1)}, bf16[512,128]{1,0:T(8,128)(2,1)S(1)}, u32[]{:S(2)}, u32[]{:S(2)}) collective-permute-start(bf16[512,128]{1,0:T(8,128)(2,1)S(1)} %copy.36), channel_id=1, source_target_pairs={{0,1},{1,2},{2,3},{3,0},{4,5},{5,6},{6,7},{7,4}} | collective-permute-start | bytes 393224 | tf_op jit(solution)/shard_map/while/body/eval_jaxpr/ppermute | solution.py:43
  61.2 5.8 %collective-permute-start.1 = (bf16[512,128]{1,0:T(8,128)(2,1)S(1)}, bf16[512,128]{1,0:T(8,128)(2,1)}, u32[]{:S(2)}, u32[]{:S(2)}) collective-permute-start(bf16[512,128]{1,0:T(8,128)(2,1)S(1)} %copy.37), channel_id=1, source_target_pairs={{0,1},{1,2},{2,3},{3,0},{4,5},{5,6},{6,7},{7,4}} | collective-permute-start | bytes 393224 | tf_op jit(solution)/shard_map/while/body/eval_jaxpr/ppermute | solution.py:44
  66.9 11.1 %collective-permute-start.5 = (bf16[512,128]{1,0:T(8,128)(2,1)S(1)}, bf16[512,128]{1,0:T(8,128)(2,1)S(1)}, u32[]{:S(2)}, u32[]{:S(2)}) collective-permute-start(bf16[512,128]{1,0:T(8,128)(2,1)S(1)} %convert.12), channel_id=1, source_target_pairs={{0,1},{1,2},{2,3},{3,0},{4,5},{5,6},{6,7},{7,4}} | collective-permute-start | bytes 393224 | tf_op jit(solution)/shard_map/ppermute | solution.py:54
  70.1 10.7 %collective-permute-start.4 = (f32[512,128]{1,0:T(8,128)S(1)}, f32[512,128]{1,0:T(8,128)S(1)}, u32[]{:S(2)}, u32[]{:S(2)}) collective-permute-start(f32[512,128]{1,0:T(8,128)S(1)} %get-tuple-element.274), channel_id=1, source_target_pairs={{0,1},{1,2},{2,3},{3,0},{4,5},{5,6},{6,7},{7,4}} | collective-permute-start | bytes 786440 | tf_op jit(solution)/shard_map/ppermute | solution.py:53
where the time goes:
time: 82.5 us; the launch traced here: 82.1 us
  starting transfers between devices  34.6 us (42%)
  waiting for transfers between devices  28.1 us (34%)
  matrix products  8.72 us (11%)
  local copies, waits for them, and re-layouts  6.14 us (7%)
  other arithmetic  3.68 us (4%)
    ppermute x3, starting transfers between devices, step_fn(): dv_next = lax.ppermute(dv_acc, 'cp', forward_perm)  16.5 us
    ppermute x3, starting transfers between devices, step_fn(): dk_next = lax.ppermute(dk_acc, 'cp', forward_perm)  12.2 us
    ppermute x3, waiting for transfers between devices, step_fn(): dv_next = lax.ppermute(dv_acc, 'cp', forward_perm)  6.66 us
    ppermute x3, waiting for transfers between devices, step_fn(): k_next = lax.ppermute(k_cur, 'cp', forward_perm)  5.95 us
    ppermute x1, waiting for transfers between devices, local_fn(): dv_home = lax.ppermute(dv_acc, 'cp', forward_perm)  4.38 us
    ppermute x3, waiting for transfers between devices, step_fn(): v_next = lax.ppermute(v_cur, 'cp', forward_perm)  4.21 us
    ppermute x3, waiting for transfers between devices, step_fn(): dk_next = lax.ppermute(dk_acc, 'cp', forward_perm)  4.11 us
    ppermute x1, starting transfers between devices, local_fn(): dv_home = lax.ppermute(dv_acc, 'cp', forward_perm)  3.14 us
  transfers between devices with their start and end apart: 14, of which 13 were waited for; matrix products, arithmetic and copies ran while one was open for 1% of the time, Pallas kernels for 0%

commit v1 on v0

v1 whole, which is shorter than its diff:
```python
import functools

import jax
import jax.numpy as jnp
from jax import lax
from jax.experimental import pallas as pl
from jax.experimental.pallas import tpu as pltpu
from jax.sharding import PartitionSpec as P

F32 = jnp.float32
BF16 = jnp.bfloat16
MESH = pl.DeviceIdType.MESH
T = 512
G = 6
E = 128
W = 256
SCALE = E ** -0.5
LOG2E = 1.4426950408889634


def dot(a, b, ca, cb):
    return lax.dot_general(a, b, (((ca,), (cb,)), ((), ())), preferred_element_type=F32)


def kernel(q_hbm, k_hbm, v_hbm, o_hbm, do_hbm, lse_hbm, gq_ref, gk_ref, gv_ref,
           q_v, do_v, o_v, lse_v, lcol, dcol, kv, acc, dq, dqr, lr, cr, fr, ld, ss, rs):
    dp = lax.axis_index('dp')
    me = lax.axis_index('cp')
    chip = me // 2
    odd = me - 2 * chip
    even_dev = 2 * chip
    odd_dev = 2 * chip + 1

    def rcopy(i, src, dst, dev):
        return pltpu.make_async_remote_copy(src, dst, ss.at[i], rs.at[i], device_id=(dp, dev), device_id_type=MESH)

    loads = []
    for c in range(2):
        for n, ref in enumerate((k_hbm, v_hbm)):
            loads.append(pltpu.make_async_copy(ref.at[pl.ds(c * W, W)], kv.at[2 * me + c, n], ld.at[2 * c + n]))
    loads.append(pltpu.make_async_copy(lse_hbm, lse_v.at[0], ld.at[4]))
    for n, (ref, buf) in enumerate(((do_hbm, do_v), (o_hbm, o_v), (q_hbm, q_v))):
        loads.append(pltpu.make_async_copy(ref, buf.at[pl.ds(0, G * T)], ld.at[5 + n]))
    for cp in loads:
        cp.start()

    bar = pltpu.get_barrier_semaphore()
    for d in range(1, 4):
        pl.semaphore_signal(bar, 1, device_id=(dp, lax.rem(me + d, 4)), device_id_type=MESH)
    pl.semaphore_wait(bar, 3)

    own = pl.ds(2 * me, 2)
    even_kv = pl.ds(2 * even_dev, 2)
    HALF = pl.ds(G * T // 2, G * T // 2)
    MOVED = pl.ds(G * T, G * T // 2)

    kv_pair = rcopy(0, kv.at[even_kv], kv.at[even_kv], odd_dev)
    q_moved = rcopy(1, q_hbm.at[HALF], q_v.at[MOVED], even_dev)
    do_moved = rcopy(2, do_hbm.at[HALF], do_v.at[MOVED], even_dev)
    o_moved = rcopy(3, o_hbm.at[HALF], o_v.at[MOVED], even_dev)
    lse_moved = rcopy(4, lse_hbm, lse_v.at[1], even_dev)
    kv_x = [rcopy(5 + j, kv.at[pl.ds(2 * j, 2)], kv.at[pl.ds(2 * j, 2)], 3) for j in range(2)]
    kv_f = [rcopy(7 + j, kv.at[pl.ds(2 * j, 2)], kv.at[pl.ds(2 * j, 2)], 2) for j in range(2)]
    dq_back = rcopy(9, dq.at[MOVED], dqr, odd_dev)
    local_back = rcopy(10, acc.at[even_kv], lr, even_dev)
    chip_sum = [rcopy(11 + j, acc.at[pl.ds(2 * j, 2)], cr.at[j], 3) for j in range(2)]
    cross_back = [rcopy(13 + j, acc.at[pl.ds(2 * j, 2)], fr, j) for j in range(2)]

    @pl.when(odd == 1)
    def _():
        do_moved.start()
        o_moved.start()
        lse_moved.start()
        q_moved.start()

    for cp in loads[:4]:
        cp.wait()

    @pl.when(odd == 0)
    def _():
        kv_pair.start()

    @pl.when(me == 0)
    def _():
        kv_x[0].start()

    acc[...] = jnp.zeros_like(acc)
    dq[...] = jnp.zeros_like(dq)
    for cp in loads[4:]:
        cp.wait()

    @pl.when(odd == 0)
    def _():
        do_moved.wait_recv()
        o_moved.wait_recv()
        lse_moved.wait_recv()
        q_moved.wait_recv()

    @pl.when(odd == 1)
    def _():
        lse_v[1, 3:6, :] = lse_v[0, 0:3, :]
        kv_pair.wait_recv()

    def rows_setup(slot, head, rows):
        lse_col = jnp.transpose(lse_v[slot, :, :])[:, head:head + 1] * LOG2E
        delta = jnp.sum(do_v[rows, :].astype(F32) * o_v[rows, :].astype(F32), axis=1, keepdims=True)
        lcol[rows, :] = lse_col
        dcol[rows, :] = delta
        return lse_col, delta

    def scores(q, do, k, v, lse_col, delta, mask=None):
        p = jnp.exp2(dot(q, k, 1, 1) * (SCALE * LOG2E) - lse_col)
        if mask is not None:
            p = jnp.where(mask, p, 0.0)
        ds = p * (dot(do, v, 1, 1) - delta)
        return p.astype(BF16), ds.astype(BF16)

    def full_step(row0, heads, g0, setup_slot=None, head0=0):
        k = jnp.concatenate([kv[g0, 0], kv[g0 + 1, 0]], axis=0)
        v = jnp.concatenate([kv[g0, 1], kv[g0 + 1, 1]], axis=0)
        for h in range(heads):
            rows = pl.ds(pl.multiple_of(row0 + h * T, T), T)
            if setup_slot is None:
                lse_col, delta = lcol[rows, :], dcol[rows, :]
            else:
                lse_col, delta = rows_setup(setup_slot, head0 + h, rows)
            q, do = q_v[rows, :], do_v[rows, :]
            p, ds = scores(q, do, k, v, lse_col, delta)
            dv = dot(do, p, 0, 0)
            dk = dot(q, ds, 0, 0)
            for c in range(2):
                acc[g0 + c, 0] += dk[:, c * W:(c + 1) * W]
                acc[g0 + c, 1] += dv[:, c * W:(c + 1) * W]
            dq[rows, :] += dot(ds, k, 1, 0)

    def diag_step():
        g0 = 2 * me
        k0, k1, v0, v1 = kv[g0, 0], kv[g0 + 1, 0], kv[g0, 1], kv[g0 + 1, 1]
        row_i = lax.broadcasted_iota(jnp.int32, (T, W), 0)
        col_i = lax.broadcasted_iota(jnp.int32, (T, W), 1)
        mask = col_i <= row_i
        for h in range(G):
            rows = pl.ds(h * T, T)
            low = pl.ds(h * T + W, W)
            lse_col, delta = rows_setup(0, h, rows)
            q, do = q_v[rows, :], do_v[rows, :]
            p0, ds0 = scores(q, do, k0, v0, lse_col, delta, mask)
            p1, ds1 = scores(q[W:], do[W:], k1, v1, lse_col[W:], delta[W:], mask[:W])
            acc[g0, 0] += dot(q, ds0, 0, 0)
            acc[g0, 1] += dot(do, p0, 0, 0)
            acc[g0 + 1, 0] += dot(q[W:], ds1, 0, 0)
            acc[g0 + 1, 1] += dot(do[W:], p1, 0, 0)
            dq[rows, :] += dot(ds0, k0, 1, 0)
            dq[low, :] += dot(ds1, k1, 1, 0)

    full_step((1 - odd) * (G * T), G // 2, 2 * even_dev, setup_slot=1, head0=3)

    @pl.when(odd == 0)
    def _():
        dq_back.start()

    @pl.when(odd == 1)
    def _():
        local_back.start()

    @pl.when(me == 1)
    def _():
        kv_x[1].start()

    diag_step()

    @pl.when(chip == 1)
    def _():
        for j in range(2):
            @pl.when(odd == 1)
            def _():
                kv_x[j].wait_recv()
                kv_f[j].start()

            @pl.when(odd == 0)
            def _():
                kv_f[j].wait_recv()

            full_step(0, G, 2 * j)

            @pl.when(odd == 0)
            def _():
                chip_sum[j].start()

            @pl.when(odd == 1)
            def _():
                chip_sum[j].wait_recv()
                acc[2 * j:2 * j + 2] += cr[j]
                cross_back[j].start()

    @pl.when(odd == 1)
    def _():
        dq_back.wait_recv()
        dq[HALF, :] += dqr[...]

    gq_ref[...] = (dq[0:G * T, :] * SCALE).astype(BF16)

    @pl.when(odd == 0)
    def _():
        local_back.wait_recv()
        acc[own] += lr[...]

    @pl.when(me == 0)
    def _():
        cross_back[0].wait_recv()

    @pl.when(me == 1)
    def _():
        cross_back[1].wait_recv()

    @pl.when(chip == 0)
    def _():
        acc[own] += fr[...]

    for c in range(2):
        gk_ref[c * W:(c + 1) * W, :] = jnp.transpose(acc[2 * me + c, 0] * SCALE).astype(BF16)
        gv_ref[c * W:(c + 1) * W, :] = jnp.transpose(acc[2 * me + c, 1]).astype(BF16)

    @pl.when(odd == 0)
    def _():
        kv_pair.wait_send()
        dq_back.wait_send()

    @pl.when(odd == 1)
    def _():
        for cp in (q_moved, do_moved, o_moved, lse_moved, local_back):
            cp.wait_send()

    @pl.when(me == 0)
    def _():
        kv_x[0].wait_send()

    @pl.when(me == 1)
    def _():
        kv_x[1].wait_send()

    @pl.when(me == 2)
    def _():
        for j in range(2):
            chip_sum[j].wait_send()

    @pl.when(me == 3)
    def _():
        for j in range(2):
            kv_f[j].wait_send()
            cross_back[j].wait_send()


def solution(mesh):
    row_spec = P(('dp', 'cp'))
    vmem = pl.BlockSpec(memory_space=pltpu.VMEM)
    hbm = pl.BlockSpec(memory_space=pl.ANY)
    ext = G * T * 3 // 2

    def local_fn(q_tok, k_tok, v_tok, fwd_out, d_out, lse_row):
        def flat(x):
            return jnp.transpose(x, (1, 0, 2)).reshape(G * T, E)

        gq, gk, gv = pl.pallas_call(
            kernel,
            out_shape=(jax.ShapeDtypeStruct((G * T, E), BF16), jax.ShapeDtypeStruct((T, E), BF16), jax.ShapeDtypeStruct((T, E), BF16)),
            in_specs=[hbm] * 6,
            out_specs=(vmem, vmem, vmem),
            scratch_shapes=[
                pltpu.VMEM((ext, E), BF16), pltpu.VMEM((ext, E), BF16), pltpu.VMEM((ext, E), BF16),
                pltpu.VMEM((2, G, T), F32), pltpu.VMEM((ext, 1), F32), pltpu.VMEM((ext, 1), F32),
                pltpu.VMEM((8, 2, W, E), BF16), pltpu.VMEM((8, 2, E, W), F32), pltpu.VMEM((ext, E), F32),
                pltpu.VMEM((G * T // 2, E), F32), pltpu.VMEM((2, 2, E, W), F32), pltpu.VMEM((2, 2, 2, E, W), F32),
                pltpu.VMEM((2, 2, E, W), F32),
                pltpu.SemaphoreType.DMA((8,)), pltpu.SemaphoreType.DMA((15,)), pltpu.SemaphoreType.DMA((15,)),
            ],
            compiler_params=pltpu.CompilerParams(collective_id=0, has_side_effects=True, vmem_limit_bytes=60 * 2 ** 20),
            name='attention_backward',
        )(flat(q_tok), k_tok, v_tok, flat(fwd_out), flat(d_out), lse_row.T)
        return jnp.transpose(gq.reshape(G, T, E), (1, 0, 2)), gk, gv

    return jax.shard_map(local_fn, mesh=mesh, in_specs=(row_spec,) * 6, out_specs=(row_spec,) * 3, check_vma=False)
```

time: 82.5 us -> 36.4 us (0.44)
  the two profiles are of different devices: /device:TPU:0 before, /device:TPU:1 now
where the time goes in v1:
time: 36.4 us; the launch traced here: 36.2 us
  Pallas kernels  31.9 us (88%)
  local copies, waits for them, and re-layouts  3.71 us (10%)
  between operations  0.65 us (2%)
    pallas_call x1, Pallas kernels, local_fn(): pl.pallas_call(kernel, out_shape=(jax.ShapeDtypeStruct((G * T, E), BF16),...  31.9 us
    unnamed x7, local copies, waits for them, and re-layouts  3.71 us

profile of v1, /device:TPU:1, one launch (start us, length us, event | category | flops | bytes accessed | tf_op | source)
XLA Modules:
  0.0 36.2 jit_solution(5596662761233151529)
XLA Ops:
  0.6 31.9 %attention_backward.1 = (bf16[3072,128]{1,0:T(8,128)(2,1)}, bf16[512,128]{1,0:T(8,128)(2,1)}, bf16[512,128]{1,0:T(8,128)(2,1)}) custom-call(bf16[3072,128]{1,0:T(8,128)(2,1)} %bitcast.14, bf16[512,128]{1,0:T(8,128)(2,1)} %k_hbm.1, bf16[512,128]{1,0:T(8,128)(2,1)} %v_hbm.1, bf16[3072,128]{1,0:T(8,128)(2,1)} %bitcast.15, bf16[3072,128]{1,0:T(8,128)(2,1)} %bitcast.16, ...), custom_call_target="tpu_custom_call" | custom-call | tf_op jit(solution)/shard_map/attention_backward/pallas_call | solution.py:264
  32.5 0.0 copy-start.1
  32.5 2.1 %copy.12 = bf16[512,6,128]{2,0,1:T(8,128)(2,1)} copy(bf16[512,6,128]{2,0,1:T(8,128)(2,1)} %bitcast.13) | data formatting | bytes 1572864
  34.6 0.0 copy-done.1
  34.6 0.0 copy-start
  34.6 0.7 %copy.13 = bf16[512,128]{1,0:T(8,128)(2,1)} copy(bf16[512,128]{1,0:T(8,128)(2,1)S(1)} %copy-done.1) | data formatting | bytes 262144
  35.3 0.3 copy-done
  35.6 0.7 %copy.14 = bf16[512,128]{1,0:T(8,128)(2,1)} copy(bf16[512,128]{1,0:T(8,128)(2,1)S(1)} %copy-done) | data formatting | bytes 262144
Async XLA Ops:
  32.5 2.1 %copy-start.1 = (bf16[512,128]{1,0:T(8,128)(2,1)S(1)}, bf16[512,128]{1,0:T(8,128)(2,1)}, u32[]{:S(2)}) copy-start(bf16[512,128]{1,0:T(8,128)(2,1)} %get-tuple-element.13) | copy-start | bytes 393220
  34.6 1.0 %copy-start = (bf16[512,128]{1,0:T(8,128)(2,1)S(1)}, bf16[512,128]{1,0:T(8,128)(2,1)}, u32[]{:S(2)}) copy-start(bf16[512,128]{1,0:T(8,128)(2,1)} %get-tuple-element.14) | copy-start | bytes 393220

commit v2 on v1

v2 whole, which is shorter than its diff:
```python
import functools

import jax
import jax.numpy as jnp
from jax import lax
from jax.experimental import pallas as pl
from jax.experimental.pallas import tpu as pltpu
from jax.sharding import PartitionSpec as P

F32 = jnp.float32
BF16 = jnp.bfloat16
MESH = pl.DeviceIdType.MESH
T = 512
G = 6
E = 128
W = 256
SCALE = E ** -0.5
LOG2E = 1.4426950408889634


def dot(a, b, ca, cb):
    return lax.dot_general(a, b, (((ca,), (cb,)), ((), ())), preferred_element_type=F32)


def kernel(q_hbm, k_hbm, v_hbm, o_hbm, do_hbm, lse_hbm, gq_ref, gk_ref, gv_ref,
           q_v, do_v, o_v, lse_v, lcol, dcol, kv, acc, dq, dqr, lr, cr, pr, fr, fs, fb, ld, ss, rs):
    dp = lax.axis_index('dp')
    me = lax.axis_index('cp')
    chip = me // 2
    odd = me - 2 * chip
    even_dev = 2 * chip
    odd_dev = 2 * chip + 1
    scope = jax.named_scope

    def rcopy(i, src, dst, dev):
        return pltpu.make_async_remote_copy(src, dst, ss.at[i], rs.at[i], device_id=(dp, dev), device_id_type=MESH)

    loads = []
    for c in range(2):
        for n, ref in enumerate((k_hbm, v_hbm)):
            loads.append(pltpu.make_async_copy(ref.at[pl.ds(c * W, W)], kv.at[2 * me + c, n], ld.at[2 * c + n]))
    loads.append(pltpu.make_async_copy(lse_hbm, lse_v.at[0], ld.at[4]))
    for n, (ref, buf) in enumerate(((do_hbm, do_v), (o_hbm, o_v), (q_hbm, q_v))):
        loads.append(pltpu.make_async_copy(ref, buf.at[pl.ds(0, G * T)], ld.at[5 + n]))
    for cp in loads:
        cp.start()

    bar = pltpu.get_barrier_semaphore()
    for d in range(1, 4):
        pl.semaphore_signal(bar, 1, device_id=(dp, lax.rem(me + d, 4)), device_id_type=MESH)
    with scope('barrier'):
        pl.semaphore_wait(bar, 3)

    own = pl.ds(2 * me, 2)
    even_kv = pl.ds(2 * even_dev, 2)
    HALF = pl.ds(G * T // 2, G * T // 2)
    MOVED = pl.ds(G * T, G * T // 2)

    kv_pair = rcopy(0, kv.at[even_kv], kv.at[even_kv], odd_dev)
    moved = [rcopy(1, do_hbm.at[HALF], do_v.at[MOVED], even_dev), rcopy(2, o_hbm.at[HALF], o_v.at[MOVED], even_dev),
             rcopy(3, q_hbm.at[HALF], q_v.at[MOVED], even_dev), rcopy(4, lse_hbm, lse_v.at[1], even_dev)]
    kv_x = [rcopy(5 + g, kv.at[g], kv.at[g], 3) for g in range(4)]
    kv_f = [rcopy(9 + g, kv.at[g], kv.at[g], 2) for g in range(4)]
    dq_back = rcopy(13, dq.at[MOVED], dqr, odd_dev)
    local_back = rcopy(14, acc.at[even_kv], lr, even_dev)
    chip_sum = [rcopy(15 + g, acc.at[g], cr.at[g], 3) for g in range(4)]
    part = rcopy(19, acc.at[pl.ds(2, 2)], pr, 3)
    back = [rcopy(20 + g, acc.at[g], fr.at[g], 0) for g in range(2)] + [rcopy(22 + g, fs.at[g], fb.at[g], 1) for g in range(2)]

    with scope('wait_kv'):
        for cp in loads[:4]:
            cp.wait()

    @pl.when(odd == 0)
    def _():
        kv_pair.start()

    @pl.when(odd == 1)
    def _():
        for cp in moved:
            cp.start()

    @pl.when(me == 0)
    def _():
        kv_x[0].start()
        kv_x[1].start()

    with scope('zero_wait_loads'):
        acc[...] = jnp.zeros_like(acc)
        dq[...] = jnp.zeros_like(dq)
        for cp in loads[4:]:
            cp.wait()

    def rows_setup(lse_t, head, rows):
        lse_col = lse_t[:, head:head + 1]
        delta = jnp.sum(do_v[rows, :].astype(F32) * o_v[rows, :].astype(F32), axis=1, keepdims=True)
        lcol[rows, :] = lse_col
        dcol[rows, :] = delta
        return lse_col, delta

    def scores(q, do, k, v, lse_col, delta, mask=None):
        p = jnp.exp2(dot(q, k, 1, 1) * (SCALE * LOG2E) - lse_col)
        if mask is not None:
            p = jnp.where(mask, p, 0.0)
        ds = p * (dot(do, v, 1, 1) - delta)
        return p.astype(BF16), ds.astype(BF16)

    def chunk_step(g):
        k, v = kv[g, 0], kv[g, 1]
        for h in range(0, G, 2):
            rows = pl.ds(h * T, 2 * T)
            q, do = q_v[rows, :], do_v[rows, :]
            p, ds = scores(q, do, k, v, lcol[rows, :], dcol[rows, :])
            acc[g, 0] += dot(q, ds, 0, 0)
            acc[g, 1] += dot(do, p, 0, 0)
            dq[rows, :] += dot(ds, k, 1, 0)

    def pair_step(heads):
        row0 = (1 - odd) * (G * T)
        g0 = 2 * even_dev
        lse_t = jnp.transpose(lse_v[1, :, :] * LOG2E)
        k = jnp.concatenate([kv[g0, 0], kv[g0 + 1, 0]], axis=0)
        v = jnp.concatenate([kv[g0, 1], kv[g0 + 1, 1]], axis=0)
        for h in heads:
            rows = pl.ds(pl.multiple_of(row0 + h * T, T), T)
            lse_col, delta = rows_setup(lse_t, 3 + h, rows)
            q, do = q_v[rows, :], do_v[rows, :]
            p, ds = scores(q, do, k, v, lse_col, delta)
            dk = dot(q, ds, 0, 0)
            dv = dot(do, p, 0, 0)
            for c in range(2):
                acc[g0 + c, 0] += dk[:, c * W:(c + 1) * W]
                acc[g0 + c, 1] += dv[:, c * W:(c + 1) * W]
            dq[rows, :] += dot(ds, k, 1, 0)

    def diag_step():
        g0 = 2 * me
        k0, k1, v0, v1 = kv[g0, 0], kv[g0 + 1, 0], kv[g0, 1], kv[g0 + 1, 1]
        row_i = lax.broadcasted_iota(jnp.int32, (T, W), 0)
        col_i = lax.broadcasted_iota(jnp.int32, (T, W), 1)
        mask = col_i <= row_i
        lse_t = jnp.transpose(lse_v[0, :, :] * LOG2E)
        for h in range(G):
            rows = pl.ds(h * T, T)
            low = pl.ds(h * T + W, W)
            lse_col, delta = rows_setup(lse_t, h, rows)
            q, do = q_v[rows, :], do_v[rows, :]
            p0, ds0 = scores(q, do, k0, v0, lse_col, delta, mask)
            p1, ds1 = scores(q[W:], do[W:], k1, v1, lse_col[W:], delta[W:], mask[:W])
            acc[g0, 0] += dot(q, ds0, 0, 0)
            acc[g0, 1] += dot(do, p0, 0, 0)
            acc[g0 + 1, 0] += dot(q[W:], ds1, 0, 0)
            acc[g0 + 1, 1] += dot(do[W:], p1, 0, 0)
            dq[rows, :] += dot(ds0, k0, 1, 0)
            dq[low, :] += dot(ds1, k1, 1, 0)

    def return_chunk(g):
        chip_sum[g].wait_recv()
        if g < 2:
            acc[g] += cr[g]
        else:
            if g == 2:
                part.wait_recv()
            total = acc[g] + cr[g] + pr[g - 2]
            fs[g - 2, 0] = (total[0] * SCALE).astype(BF16)
            fs[g - 2, 1] = total[1].astype(BF16)
        back[g].start()

    with scope('diag'):
        diag_step()

    @pl.when(me == 1)
    def _():
        kv_x[2].start()
        kv_x[3].start()
        part.start()

    @pl.when(chip == 1)
    def _():
        for g in range(4):
            with scope('wait_x'):
                @pl.when(odd == 1)
                def _():
                    kv_x[g].wait_recv()
                    kv_f[g].start()

                @pl.when(odd == 0)
                def _():
                    kv_f[g].wait_recv()

            with scope('cross'):
                chunk_step(g)

            with scope('sum'):
                @pl.when(odd == 0)
                def _():
                    chip_sum[g].start()

                if g > 0:
                    @pl.when(odd == 1)
                    def _():
                        return_chunk(g - 1)

    with scope('wait_pair'):
        @pl.when(odd == 0)
        def _():
            for cp in moved:
                cp.wait_recv()

        @pl.when(odd == 1)
        def _():
            lse_v[1, 3:6, :] = lse_v[0, 0:3, :]
            kv_pair.wait_recv()

    with scope('pair'):
        pair_step((0, 1))

    with scope('return3'):
        @pl.when(me == 3)
        def _():
            return_chunk(3)

    with scope('pair'):
        pair_step((2,))

    @pl.when(odd == 0)
    def _():
        dq_back.start()

    @pl.when(odd == 1)
    def _():
        local_back.start()

    with scope('results'):
        @pl.when(odd == 1)
        def _():
            dq_back.wait_recv()
            dq[HALF, :] += dqr[...]

        gq_ref[...] = (dq[0:G * T, :] * SCALE).astype(BF16)

        @pl.when(odd == 0)
        def _():
            local_back.wait_recv()
            acc[own] += lr[...]

        @pl.when(me == 0)
        def _():
            back[0].wait_recv()
            back[1].wait_recv()
            acc[own] += fr[...]

        @pl.when(me == 1)
        def _():
            for c in range(2):
                back[2 + c].wait_recv()
                gk_ref[c * W:(c + 1) * W, :] = jnp.transpose(fb[c, 0])
                gv_ref[c * W:(c + 1) * W, :] = jnp.transpose(fb[c, 1])

        @pl.when(me != 1)
        def _():
            for c in range(2):
                gk_ref[c * W:(c + 1) * W, :] = jnp.transpose(acc[2 * me + c, 0] * SCALE).astype(BF16)
                gv_ref[c * W:(c + 1) * W, :] = jnp.transpose(acc[2 * me + c, 1]).astype(BF16)

    with scope('sends'):
        @pl.when(odd == 0)
        def _():
            kv_pair.wait_send()
            dq_back.wait_send()

        @pl.when(odd == 1)
        def _():
            for cp in moved + [local_back]:
                cp.wait_send()

        @pl.when(me == 0)
        def _():
            kv_x[0].wait_send()
            kv_x[1].wait_send()

        @pl.when(me == 1)
        def _():
            for cp in (kv_x[2], kv_x[3], part):
                cp.wait_send()

        @pl.when(me == 2)
        def _():
            for g in range(4):
                chip_sum[g].wait_send()

        @pl.when(me == 3)
        def _():
            for g in range(4):
                kv_f[g].wait_send()
                back[g].wait_send()


def write_out(gq_v, gk_v, gv_v, gq_hbm, gk_hbm, gv_hbm, sem):
    copies = [pltpu.make_async_copy(a, b, sem.at[i]) for i, (a, b) in enumerate(((gq_v, gq_hbm), (gk_v, gk_hbm), (gv_v, gv_hbm)))]
    for cp in copies:
        cp.start()
    for cp in copies:
        cp.wait()


def solution(mesh):
    row_spec = P(('dp', 'cp'))
    vmem = pl.BlockSpec(memory_space=pltpu.VMEM)
    hbm = pl.BlockSpec(memory_space=pltpu.HBM)
    ext = G * T * 3 // 2

    def local_fn(q_tok, k_tok, v_tok, fwd_out, d_out, lse_row):
        def flat(x):
            return jnp.transpose(x, (1, 0, 2)).reshape(G * T, E)

        results = (jax.ShapeDtypeStruct((G * T, E), BF16), jax.ShapeDtypeStruct((T, E), BF16), jax.ShapeDtypeStruct((T, E), BF16))
        staged = pl.pallas_call(
            kernel,
            out_shape=results,
            in_specs=[hbm] * 6,
            out_specs=(vmem, vmem, vmem),
            scratch_shapes=[
                pltpu.VMEM((ext, E), BF16), pltpu.VMEM((ext, E), BF16), pltpu.VMEM((ext, E), BF16),
                pltpu.VMEM((2, G, T), F32), pltpu.VMEM((ext, 1), F32), pltpu.VMEM((ext, 1), F32),
                pltpu.VMEM((8, 2, W, E), BF16), pltpu.VMEM((8, 2, E, W), F32), pltpu.VMEM((ext, E), F32),
                pltpu.VMEM((G * T // 2, E), F32), pltpu.VMEM((2, 2, E, W), F32), pltpu.VMEM((4, 2, E, W), F32),
                pltpu.VMEM((2, 2, E, W), F32), pltpu.VMEM((2, 2, E, W), F32), pltpu.VMEM((2, 2, E, W), BF16), pltpu.VMEM((2, 2, E, W), BF16),
                pltpu.SemaphoreType.DMA((8,)), pltpu.SemaphoreType.DMA((24,)), pltpu.SemaphoreType.DMA((24,)),
            ],
            compiler_params=pltpu.CompilerParams(collective_id=0, has_side_effects=True, vmem_limit_bytes=40 * 2 ** 20),
            name='attention_backward',
        )(*[pltpu.with_memory_space_constraint(x, pltpu.HBM) for x in (flat(q_tok), k_tok, v_tok, flat(fwd_out), flat(d_out), lse_row.T)])
        gq, gk, gv = pl.pallas_call(
            write_out,
            out_shape=results,
            in_specs=[vmem] * 3,
            out_specs=(hbm,) * 3,
            scratch_shapes=[pltpu.SemaphoreType.DMA((3,))],
            compiler_params=pltpu.CompilerParams(vmem_limit_bytes=4 * 2 ** 20),
            name='write_out',
        )(*staged)
        return jnp.transpose(gq.reshape(G, T, E), (1, 0, 2)), gk, gv

    return jax.shard_map(local_fn, mesh=mesh, in_specs=(row_spec,) * 6, out_specs=(row_spec,) * 3, check_vma=False)
```

time: 36.4 us -> 24 us (0.66)
  Pallas kernels: 31.9 us -> 23.1 us
  local copies, waits for them, and re-layouts: 3.71 us -> 0 us
    pallas_call x1 -> x2, Pallas kernels: 31.9 us -> 23.1 us  [the longest x1 22.1 us: local_fn(): pl.pallas_call(kernel, out_shape=results, in_specs=[hbm] * 6, out_specs=(...]
    unnamed x7 -> x0, local copies, waits for them, and re-layouts: 3.71 us -> none
where the time goes in v2:
time: 24 us; the launch traced here: 23.9 us
  Pallas kernels  23.1 us (96%)
  between operations  0.8 us (3%)
    pallas_call x1, Pallas kernels, local_fn(): pl.pallas_call(kernel, out_shape=results, in_specs=[hbm] * 6, out_specs=(...  22.1 us
    pallas_call x1, Pallas kernels, local_fn(): pl.pallas_call(write_out, out_shape=results, in_specs=[vmem] * 3, out_spe...  0.99 us

profile of v2, /device:TPU:1, one launch (start us, length us, event | category | flops | bytes accessed | tf_op | source)
XLA Modules:
  0.0 23.9 jit_solution(13675661798430306879)
XLA Ops:
  0.6 22.1 %attention_backward.1 = (bf16[3072,128]{1,0:T(8,128)(2,1)S(1)}, bf16[512,128]{1,0:T(8,128)(2,1)S(1)}, bf16[512,128]{1,0:T(8,128)(2,1)S(1)}) custom-call(bf16[3072,128]{1,0:T(8,128)(2,1)} %bitcast.13, bf16[512,128]{1,0:T(8,128)(2,1)} %k_hbm.1, bf16[512,128]{1,0:T(8,128)(2,1)} %v_hbm.1, bf16[3072,128]{1,0:T(8,128)(2,1)} %bitcast.14, ...), custom_call_target="tpu_custom_call" | custom-call | tf_op jit(solution)/shard_map/attention_backward/pallas_call | solution.py:318
  22.7 1.0 %write_out.1 = (bf16[3072,128]{1,0:T(8,128)(2,1)}, bf16[512,128]{1,0:T(8,128)(2,1)}, bf16[512,128]{1,0:T(8,128)(2,1)}) custom-call(bf16[3072,128]{1,0:T(8,128)(2,1)S(1)} %get-tuple-element.9.gq_v, bf16[512,128]{1,0:T(8,128)(2,1)S(1)} %get-tuple-element.10.gk_v, bf16[512,128]{1,0:T(8,128)(2,1)S(1)} %get-tuple-element.11.gv_v), custom_call_target="tpu_custom_call" | custom-call | tf_op jit(solution)/shard_map/write_out/pallas_call | solution.py:334

commit v3 on v2

v3 whole, which is shorter than its diff:
```python
import functools

import jax
import jax.numpy as jnp
from jax import lax
from jax.experimental import pallas as pl
from jax.experimental.pallas import tpu as pltpu
from jax.sharding import PartitionSpec as P

F32 = jnp.float32
BF16 = jnp.bfloat16
MESH = pl.DeviceIdType.MESH
T = 512
G = 6
E = 128
W = 256
SCALE = E ** -0.5
LOG2E = 1.4426950408889634


def dot(a, b, ca, cb):
    return lax.dot_general(a, b, (((ca,), (cb,)), ((), ())), preferred_element_type=F32)


def kernel(q_hbm, k_hbm, v_hbm, o_hbm, do_hbm, lse_hbm, gq_ref, gk_ref, gv_ref,
           x_v, lse_v, lcol, dcol, kv, acc, dq, dqr, lr, cr, pr, fr, fs, fb, ld, ss, rs, go):
    dp = lax.axis_index('dp')
    me = lax.axis_index('cp')
    chip = me // 2
    odd = me - 2 * chip
    even_dev = 2 * chip
    odd_dev = 2 * chip + 1
    scope = jax.named_scope
    do_v, o_v, q_v = x_v.at[0], x_v.at[1], x_v.at[2]

    def rcopy(i, j, src, dst, dev):
        return pltpu.make_async_remote_copy(src, dst, ss.at[i], rs.at[j], device_id=(dp, dev), device_id_type=MESH)

    def when(cond, *fns):
        @pl.when(cond)
        def _():
            for f in fns:
                f()

    mine = pl.ds(me * T, T)
    loads = [pltpu.make_async_copy(src, dst, ld.at[n]) for n, (src, dst) in enumerate((
        (k_hbm, kv.at[0, mine]), (v_hbm, kv.at[1, mine]), (lse_hbm, lse_v.at[0]),
        (do_hbm, do_v.at[pl.ds(0, G * T)]), (o_hbm, o_v.at[pl.ds(0, G * T)]), (q_hbm, q_v.at[pl.ds(0, G * T)])))]
    for cp in loads:
        cp.start()

    bar = pltpu.get_barrier_semaphore()

    def greet(sem, dev):
        pl.semaphore_signal(sem, 1, device_id=(dp, dev), device_id_type=MESH)

    @pl.when(me == 3)
    def _():
        for d in range(3):
            greet(bar, d)

    when(me != 3, lambda: greet(bar, 3))
    with scope('barrier'):
        when(me == 3, lambda: pl.semaphore_wait(bar, 3))
        when(me != 3, lambda: pl.semaphore_wait(bar, 1))

    @pl.when(me == 3)
    def _():
        for d in range(3):
            greet(go, d)

    own = pl.ds(2 * me, 2)
    HALF = pl.ds(G * T // 2, G * T // 2)
    MOVED = pl.ds(G * T, G * T // 2)
    even_rows = pl.ds(even_dev * T, T)

    def kv_chunk(g):
        return kv.at[:, pl.ds(g * W, W)]

    kv_pair = rcopy(0, 0, kv.at[:, even_rows], kv.at[:, even_rows], odd_dev)
    dq_back = rcopy(1, 1, dq.at[MOVED], dqr, odd_dev)
    moved = [rcopy(0, 0, lse_v.at[0], lse_v.at[1], even_dev), rcopy(1, 1, x_v.at[:, HALF], x_v.at[:, MOVED], even_dev)]
    local_back = rcopy(2, 2, acc.at[pl.ds(2 * even_dev, 2)], lr, even_dev)
    kv_x = [rcopy((2, 3, 3, 4)[g], 2 + g, kv_chunk(g), kv_chunk(g), 3) for g in range(4)]
    kv_f = [rcopy(3 + g % 2, 3 + g, kv_chunk(g), kv_chunk(g), 2) for g in range(4)]
    chip_sum = [rcopy(5 + g % 2, 7 + g, acc.at[g], cr.at[g], 2) for g in range(4)]
    part = [rcopy(5 + c, 11 + c, acc.at[2 + c], pr.at[c], 2) for c in range(2)]
    back = [rcopy(2 + g, 3 + g, acc.at[g], fr.at[g], 0) for g in range(2)]
    back += [rcopy(4 + c, 2 + c, fs.at[c], fb.at[c], 1) for c in range(2)]

    with scope('wait_kv'):
        loads[0].wait()
        loads[1].wait()

    when(me == 0, kv_x[0].start, kv_x[1].start)

    with scope('zero_wait_loads'):
        acc[...] = jnp.zeros_like(acc)
        zeros = pl.ds(4 * T, (G - 4) * T + G * T // 2)
        dq[zeros, :] = jnp.zeros((zeros.size, E), F32)
        for cp in loads[2:]:
            cp.wait()

    def rows_setup(lse_t, head, rows):
        lcol[rows, :] = jnp.broadcast_to(lse_t[:, head:head + 1], (T, E))
        delta = jnp.sum(do_v[rows, :].astype(F32) * o_v[rows, :].astype(F32), axis=1, keepdims=True)
        dcol[rows, :] = jnp.broadcast_to(delta, (T, E))

    def scores(q, do, k, v, lse_col, delta, mask=None):
        n = k.shape[0] // E
        p = jnp.exp2(dot(q, k, 1, 1) * (SCALE * LOG2E) - jnp.concatenate([lse_col] * n, axis=1))
        if mask is not None:
            step = p.shape[0] // 2
            p = jnp.concatenate([x for i in range(0, 2 * step, step)
                                 for x in (jnp.where(mask, p[i:i + W], 0.0), p[i + W:i + step])[:step // W]], axis=0)
        ds = p * (dot(do, v, 1, 1) - jnp.concatenate([delta] * n, axis=1))
        return p.astype(BF16), ds.astype(BF16)

    def chunk_step(g):
        cols = pl.ds(g * W, W)
        k, v = kv[0, cols, :], kv[1, cols, :]
        blocks = [pl.ds(h * T, 2 * T) for h in range(0, G, 2)]
        done = [scores(q_v[rows, :], do_v[rows, :], k, v, lcol[rows, :], dcol[rows, :]) for rows in blocks]
        for rows, (p, ds) in zip(blocks, done):
            dq[rows, :] += dot(ds, k, 1, 0)
            acc[g, 0] += dot(q_v[rows, :], ds, 0, 0)
            acc[g, 1] += dot(do_v[rows, :], p, 0, 0)

    def pair_step(heads):
        row0 = (1 - odd) * (G * T)
        g0 = 2 * even_dev
        lse_t = jnp.transpose(lse_v[1, :, :] * LOG2E)
        k, v = kv[0, even_rows, :], kv[1, even_rows, :]
        blocks = [pl.ds(pl.multiple_of(row0 + h * T, T), T) for h in heads]
        for h, rows in zip(heads, blocks):
            rows_setup(lse_t, 3 + h, rows)
        done = [scores(q_v[rows, :], do_v[rows, :], k, v, lcol[rows, :], dcol[rows, :]) for rows in blocks]
        for rows, (p, ds) in zip(blocks, done):
            dq[rows, :] += dot(ds, k, 1, 0)
            dk = dot(q_v[rows, :], ds, 0, 0)
            dv = dot(do_v[rows, :], p, 0, 0)
            for c in range(2):
                acc[g0 + c, 0] += dk[:, c * W:(c + 1) * W]
                acc[g0 + c, 1] += dv[:, c * W:(c + 1) * W]

    def diag_step(heads, setup_heads):
        g0 = 2 * me
        k, v = kv[0, mine, :], kv[1, mine, :]
        row_i = lax.broadcasted_iota(jnp.int32, (W, W), 0)
        col_i = lax.broadcasted_iota(jnp.int32, (W, W), 1)
        mask = col_i <= row_i
        if setup_heads:
            lse_t = jnp.transpose(lse_v[0, :, :] * LOG2E)

        def low(x):
            return jnp.concatenate([x[W:T], x[T + W:]], axis=0)

        for h in heads:
            if setup_heads:
                for i in range(2):
                    rows_setup(lse_t, h + i, pl.ds((h + i) * T, T))
            rows = pl.ds(h * T, 2 * T)
            lse_col, delta = lcol[rows, :], dcol[rows, :]
            q, do = q_v[rows, :], do_v[rows, :]
            p0, ds0 = scores(q, do, k[:W], v[:W], lse_col, delta, mask)
            q1, do1 = low(q), low(do)
            p1, ds1 = scores(q1, do1, k[W:], v[W:], low(lse_col), low(delta), mask)
            dq0, dq1 = dot(ds0, k[:W], 1, 0), dot(ds1, k[W:], 1, 0)
            new = [x for i in range(2) for x in (dq0[i * T:i * T + W], dq0[i * T + W:(i + 1) * T] + dq1[i * W:(i + 1) * W])]
            if h < 4:
                dq[rows, :] = jnp.concatenate(new, axis=0)
            else:
                dq[rows, :] += jnp.concatenate(new, axis=0)
            acc[g0, 0] += dot(q, ds0, 0, 0)
            acc[g0, 1] += dot(do, p0, 0, 0)
            acc[g0 + 1, 0] += dot(q1, ds1, 0, 0)
            acc[g0 + 1, 1] += dot(do1, p1, 0, 0)
        for h in range(max(heads) + 2, setup_heads):
            rows_setup(lse_t, h, pl.ds(h * T, T))

    def return_chunk(g):
        chip_sum[g].wait_recv()
        if g < 2:
            acc[g] += cr[g]
        else:
            part[g - 2].wait_recv()
            total = acc[g] + cr[g] + pr[g - 2]
            fs[g - 2, 0] = (total[0] * SCALE).astype(BF16)
            fs[g - 2, 1] = total[1].astype(BF16)
        back[g].start()

    with scope('diag_a'):
        diag_step((0, 2), G)

    with scope('go'):
        when(me != 3, lambda: pl.semaphore_wait(go, 1))

    when(me == 1, kv_x[2].start, kv_x[3].start)
    when(odd == 0, kv_pair.start)
    when(me == 1, moved[0].start, moved[1].start)

    with scope('diag_b'):
        when(me != 3, lambda: diag_step((4,), 0))

    when(me == 1, part[0].start, part[1].start)

    def forward(g):
        kv_x[g].wait_recv()
        if g >= 2:
            kv_f[g - 2].wait_send()
        kv_f[g].start()

    def send_sum(g):
        if g >= 2:
            chip_sum[g - 2].wait_send()
        chip_sum[g].start()

    @pl.when(chip == 1)
    def _():
        with scope('wait_x'):
            when(odd == 1, lambda: forward(0), moved[0].start, moved[1].start)
        for g in range(4):
            with scope('wait_f'):
                when(odd == 0, kv_f[g].wait_recv)
            with scope('cross'):
                chunk_step(g)
            with scope('sum'):
                @pl.when(odd == 1)
                def _():
                    send_sum(g)
                    if g < 3:
                        forward(g + 1)

                if g < 3:
                    when(odd == 0, lambda: return_chunk(g))

        with scope('diag_b'):
            when(odd == 1, lambda: diag_step((4,), 0))

    with scope('wait_pair'):
        when(odd == 0, moved[0].wait_recv, moved[1].wait_recv)

        @pl.when(odd == 1)
        def _():
            lse_v[1, 3:6, :] = lse_v[0, 0:3, :]
            kv_pair.wait_recv()

    with scope('pair'):
        pair_step((0,))

    with scope('return3'):
        when(me == 2, lambda: return_chunk(3))

    with scope('pair'):
        pair_step((1, 2))

    when(odd == 0, dq_back.start)
    when(odd == 1, local_back.start)

    with scope('results'):
        @pl.when(odd == 1)
        def _():
            dq_back.wait_recv()
            dq[HALF, :] += dqr[...]

        gq_ref[...] = (dq[0:G * T, :] * SCALE).astype(BF16)

        @pl.when(odd == 0)
        def _():
            local_back.wait_recv()
            acc[own] += lr[...]

        @pl.when(me == 0)
        def _():
            back[0].wait_recv()
            back[1].wait_recv()
            acc[own] += fr[...]

        @pl.when(me == 1)
        def _():
            for c in range(2):
                back[2 + c].wait_recv()
                gk_ref[c * W:(c + 1) * W, :] = jnp.transpose(fb[c, 0])
                gv_ref[c * W:(c + 1) * W, :] = jnp.transpose(fb[c, 1])

        @pl.when(me != 1)
        def _():
            for c in range(2):
                gk_ref[c * W:(c + 1) * W, :] = jnp.transpose(acc[2 * me + c, 0] * SCALE).astype(BF16)
                gv_ref[c * W:(c + 1) * W, :] = jnp.transpose(acc[2 * me + c, 1]).astype(BF16)

    with scope('sends'):
        when(odd == 0, kv_pair.wait_send, dq_back.wait_send)
        when(odd == 1, moved[0].wait_send, moved[1].wait_send, local_back.wait_send)
        when(me == 0, kv_x[0].wait_send, kv_x[1].wait_send)
        when(me == 1, kv_x[2].wait_send, kv_x[3].wait_send, part[0].wait_send, part[1].wait_send)
        when(me == 2, *(cp.wait_send for cp in back))
        when(me == 3, kv_f[2].wait_send, kv_f[3].wait_send, chip_sum[2].wait_send, chip_sum[3].wait_send)


def write_out(gq_v, gk_v, gv_v, gq_hbm, gk_hbm, gv_hbm, sem):
    pieces = [pl.ds(i * 2 * T, 2 * T) for i in range(G // 2)]
    pairs = [(gq_v.at[r], gq_hbm.at[r]) for r in pieces] + [(gk_v, gk_hbm), (gv_v, gv_hbm)]
    copies = [pltpu.make_async_copy(a, b, sem.at[i]) for i, (a, b) in enumerate(pairs)]
    for cp in copies:
        cp.start()
    for cp in copies:
        cp.wait()


def solution(mesh):
    row_spec = P(('dp', 'cp'))
    vmem = pl.BlockSpec(memory_space=pltpu.VMEM)
    hbm = pl.BlockSpec(memory_space=pltpu.HBM)
    ext = G * T * 3 // 2

    def local_fn(q_tok, k_tok, v_tok, fwd_out, d_out, lse_row):
        def flat(x):
            return jnp.transpose(x, (1, 0, 2)).reshape(G * T, E)

        results = (jax.ShapeDtypeStruct((G * T, E), BF16), jax.ShapeDtypeStruct((T, E), BF16), jax.ShapeDtypeStruct((T, E), BF16))
        staged = pl.pallas_call(
            kernel,
            out_shape=results,
            in_specs=[hbm] * 6,
            out_specs=(vmem, vmem, vmem),
            scratch_shapes=[
                pltpu.VMEM((3, ext, E), BF16), pltpu.VMEM((2, G, T), F32), pltpu.VMEM((ext, E), F32), pltpu.VMEM((ext, E), F32),
                pltpu.VMEM((2, 4 * T, E), BF16), pltpu.VMEM((8, 2, E, W), F32), pltpu.VMEM((ext, E), F32),
                pltpu.VMEM((G * T // 2, E), F32), pltpu.VMEM((2, 2, E, W), F32), pltpu.VMEM((4, 2, E, W), F32),
                pltpu.VMEM((2, 2, E, W), F32), pltpu.VMEM((2, 2, E, W), F32),
                pltpu.VMEM((2, 2, E, W), BF16), pltpu.VMEM((2, 2, E, W), BF16),
                pltpu.SemaphoreType.DMA((6,)), pltpu.SemaphoreType.DMA((7,)), pltpu.SemaphoreType.DMA((13,)), pltpu.SemaphoreType.REGULAR,
            ],
            compiler_params=pltpu.CompilerParams(collective_id=0, has_side_effects=True, vmem_limit_bytes=40 * 2 ** 20),
            name='attention_backward',
        )(*[pltpu.with_memory_space_constraint(x, pltpu.HBM) for x in (flat(q_tok), k_tok, v_tok, flat(fwd_out), flat(d_out), lse_row.T)])
        gq, gk, gv = pl.pallas_call(
            write_out,
            out_shape=results,
            in_specs=[vmem] * 3,
            out_specs=(hbm,) * 3,
            scratch_shapes=[pltpu.SemaphoreType.DMA((2 + G // 2,))],
            compiler_params=pltpu.CompilerParams(vmem_limit_bytes=4 * 2 ** 20),
            name='write_out',
        )(*staged)
        return jnp.transpose(gq.reshape(G, T, E), (1, 0, 2)), gk, gv

    return jax.shard_map(local_fn, mesh=mesh, in_specs=(row_spec,) * 6, out_specs=(row_spec,) * 3, check_vma=False)
```

time: 24 us -> 21.6 us (0.900)
  Pallas kernels: 23.1 us -> 20.9 us
    pallas_call x1, Pallas kernels: 22.1 us -> 19.9 us  [local_fn(): pl.pallas_call(kernel, out_shape=results, in_specs=[hbm] * 6, out_specs=(...]
where the time goes in v3:
time: 21.6 us; the launch traced here: 21.5 us
  Pallas kernels  20.9 us (97%)
  between operations  0.64 us (3%)
    pallas_call x1, Pallas kernels, local_fn(): pl.pallas_call(kernel, out_shape=results, in_specs=[hbm] * 6, out_specs=(...  19.9 us
    pallas_call x1, Pallas kernels, local_fn(): pl.pallas_call(write_out, out_shape=results, in_specs=[vmem] * 3, out_spe...  1 us

profile of v3, /device:TPU:1, one launch (start us, length us, event | category | flops | bytes accessed | tf_op | source)
XLA Modules:
  0.0 21.5 jit_solution(17524559818719723709)
XLA Ops:
  0.6 19.9 %attention_backward.1 = (bf16[3072,128]{1,0:T(8,128)(2,1)S(1)}, bf16[512,128]{1,0:T(8,128)(2,1)S(1)}, bf16[512,128]{1,0:T(8,128)(2,1)S(1)}) custom-call(bf16[3072,128]{1,0:T(8,128)(2,1)} %bitcast.13, bf16[512,128]{1,0:T(8,128)(2,1)} %k_hbm.1, bf16[512,128]{1,0:T(8,128)(2,1)} %v_hbm.1, bf16[3072,128]{1,0:T(8,128)(2,1)} %bitcast.14, ...), custom_call_target="tpu_custom_call" | custom-call | tf_op jit(solution)/shard_map/attention_backward/pallas_call | solution.py:322
  20.5 1.0 %write_out.1 = (bf16[3072,128]{1,0:T(8,128)(2,1)}, bf16[512,128]{1,0:T(8,128)(2,1)}, bf16[512,128]{1,0:T(8,128)(2,1)}) custom-call(bf16[3072,128]{1,0:T(8,128)(2,1)S(1)} %get-tuple-element.9.gq_v, bf16[512,128]{1,0:T(8,128)(2,1)S(1)} %get-tuple-element.10.gk_v, bf16[512,128]{1,0:T(8,128)(2,1)S(1)} %get-tuple-element.11.gv_v), custom_call_target="tpu_custom_call" | custom-call | tf_op jit(solution)/shard_map/write_out/pallas_call | solution.py:338

commit v4 on v3

--- a/solution.py
+++ b/solution.py
@@ -83,10 +83,13 @@
     local_back = rcopy(2, 2, acc.at[pl.ds(2 * even_dev, 2)], lr, even_dev)
     kv_x = [rcopy((2, 3, 3, 4)[g], 2 + g, kv_chunk(g), kv_chunk(g), 3) for g in range(4)]
     kv_f = [rcopy(3 + g % 2, 3 + g, kv_chunk(g), kv_chunk(g), 2) for g in range(4)]
-    chip_sum = [rcopy(5 + g % 2, 7 + g, acc.at[g], cr.at[g], 2) for g in range(4)]
-    part = [rcopy(5 + c, 11 + c, acc.at[2 + c], pr.at[c], 2) for c in range(2)]
-    back = [rcopy(2 + g, 3 + g, acc.at[g], fr.at[g], 0) for g in range(2)]
-    back += [rcopy(4 + c, 2 + c, fs.at[c], fb.at[c], 1) for c in range(2)]
+    first_sum = [rcopy(5 + 2 * n, 7 + 2 * n, acc.at[0, n], cr.at[0, n], 2) for n in range(2)]
+    chip_sum = [None, rcopy(6, 8, acc.at[1], cr.at[1], 2)]
+    chip_sum += [rcopy(2 + g, 4 + g, acc.at[g], cr.at[g], 3) for g in range(2, 4)]
+    part = [rcopy(5 + c, 8 + c, acc.at[2 + c], pr.at[c], 3) for c in range(2)]
+    first_back = [rcopy(2 + 4 * n, 3 + 2 * n, acc.at[0, n], fr.at[0, n], 0) for n in range(2)]
+    back = [None, rcopy(3, 4, acc.at[1], fr.at[1], 0)]
+    back += [rcopy(5 + c, 2 + c, fs.at[c], fb.at[c], 1) for c in range(2)]
 
     with scope('wait_kv'):
         loads[0].wait()
@@ -179,14 +182,21 @@
             rows_setup(lse_t, h, pl.ds(h * T, T))
 
     def return_chunk(g):
+        if g == 0:
+            for n in range(2):
+                first_sum[n].wait_recv()
+                acc[0, n] += cr[0, n]
+                first_back[n].start()
+            return
         chip_sum[g].wait_recv()
-        if g < 2:
+        if g == 1:
             acc[g] += cr[g]
         else:
             part[g - 2].wait_recv()
             total = acc[g] + cr[g] + pr[g - 2]
             fs[g - 2, 0] = (total[0] * SCALE).astype(BF16)
             fs[g - 2, 1] = total[1].astype(BF16)
+            (first_sum[0] if g == 2 else chip_sum[1]).wait_send()
         back[g].start()
 
     with scope('diag_a'):
@@ -195,25 +205,19 @@
     with scope('go'):
         when(me != 3, lambda: pl.semaphore_wait(go, 1))
 
-    when(me == 1, kv_x[2].start, kv_x[3].start)
     when(odd == 0, kv_pair.start)
     when(me == 1, moved[0].start, moved[1].start)
 
     with scope('diag_b'):
         when(me != 3, lambda: diag_step((4,), 0))
 
-    when(me == 1, part[0].start, part[1].start)
+    when(me == 1, kv_x[2].start, kv_x[3].start, part[0].start, part[1].start)
 
     def forward(g):
         kv_x[g].wait_recv()
         if g >= 2:
             kv_f[g - 2].wait_send()
         kv_f[g].start()
-
-    def send_sum(g):
-        if g >= 2:
-            chip_sum[g - 2].wait_send()
-        chip_sum[g].start()
 
     @pl.when(chip == 1)
     def _():
@@ -225,17 +229,20 @@
             with scope('cross'):
                 chunk_step(g)
             with scope('sum'):
-                @pl.when(odd == 1)
-                def _():
-                    send_sum(g)
-                    if g < 3:
-                        forward(g + 1)
-
-                if g < 3:
+                if g < 2:
+                    when(odd == 1, *(cp.start for cp in (chip_sum[1:2] if g else first_sum)), lambda: forward(g + 1))
                     when(odd == 0, lambda: return_chunk(g))
-
-        with scope('diag_b'):
-            when(odd == 1, lambda: diag_step((4,), 0))
+                else:
+                    when(odd == 0, chip_sum[g].start)
+            if g == 1:
+                with scope('diag_b'):
+                    @pl.when(odd == 1)
+                    def _():
+                        diag_step((4,), 0)
+                        forward(3)
+
+        with scope('return2'):
+            when(odd == 1, lambda: return_chunk(2))
 
     with scope('wait_pair'):
         when(odd == 0, moved[0].wait_recv, moved[1].wait_recv)
@@ -249,7 +256,7 @@
         pair_step((0,))
 
     with scope('return3'):
-        when(me == 2, lambda: return_chunk(3))
+        when(me == 3, lambda: return_chunk(3))
 
     with scope('pair'):
         pair_step((1, 2))
@@ -272,8 +279,8 @@
 
         @pl.when(me == 0)
         def _():
-            back[0].wait_recv()
-            back[1].wait_recv()
+            for cp in first_back + back[1:2]:
+                cp.wait_recv()
             acc[own] += fr[...]
 
         @pl.when(me == 1)
@@ -294,13 +301,12 @@
         when(odd == 1, moved[0].wait_send, moved[1].wait_send, local_back.wait_send)
         when(me == 0, kv_x[0].wait_send, kv_x[1].wait_send)
         when(me == 1, kv_x[2].wait_send, kv_x[3].wait_send, part[0].wait_send, part[1].wait_send)
-        when(me == 2, *(cp.wait_send for cp in back))
-        when(me == 3, kv_f[2].wait_send, kv_f[3].wait_send, chip_sum[2].wait_send, chip_sum[3].wait_send)
+        when(me == 2, *(cp.wait_send for cp in first_back + back[1:2] + chip_sum[2:]))
+        when(me == 3, *(cp.wait_send for cp in kv_f[2:] + first_sum[1:] + back[2:]))
 
 
 def write_out(gq_v, gk_v, gv_v, gq_hbm, gk_hbm, gv_hbm, sem):
-    pieces = [pl.ds(i * 2 * T, 2 * T) for i in range(G // 2)]
-    pairs = [(gq_v.at[r], gq_hbm.at[r]) for r in pieces] + [(gk_v, gk_hbm), (gv_v, gv_hbm)]
+    pairs = [(gq_v, gq_hbm), (gk_v, gk_hbm), (gv_v, gv_hbm)]
     copies = [pltpu.make_async_copy(a, b, sem.at[i]) for i, (a, b) in enumerate(pairs)]
     for cp in copies:
         cp.start()
@@ -330,7 +336,7 @@
                 pltpu.VMEM((G * T // 2, E), F32), pltpu.VMEM((2, 2, E, W), F32), pltpu.VMEM((4, 2, E, W), F32),
                 pltpu.VMEM((2, 2, E, W), F32), pltpu.VMEM((2, 2, E, W), F32),
                 pltpu.VMEM((2, 2, E, W), BF16), pltpu.VMEM((2, 2, E, W), BF16),
-                pltpu.SemaphoreType.DMA((6,)), pltpu.SemaphoreType.DMA((7,)), pltpu.SemaphoreType.DMA((13,)), pltpu.SemaphoreType.REGULAR,
+                pltpu.SemaphoreType.DMA((6,)), pltpu.SemaphoreType.DMA((8,)), pltpu.SemaphoreType.DMA((10,)), pltpu.SemaphoreType.REGULAR,
             ],
             compiler_params=pltpu.CompilerParams(collective_id=0, has_side_effects=True, vmem_limit_bytes=40 * 2 ** 20),
             name='attention_backward',
@@ -340,7 +346,7 @@
             out_shape=results,
             in_specs=[vmem] * 3,
             out_specs=(hbm,) * 3,
-            scratch_shapes=[pltpu.SemaphoreType.DMA((2 + G // 2,))],
+            scratch_shapes=[pltpu.SemaphoreType.DMA((3,))],
             compiler_params=pltpu.CompilerParams(vmem_limit_bytes=4 * 2 ** 20),
             name='write_out',
         )(*staged)

time: 21.6 us -> 21.5 us (level)
  Pallas kernels: 20.9 us -> 20.6 us
    pallas_call x1, Pallas kernels: 19.9 us -> 19.6 us  [local_fn(): pl.pallas_call(kernel, out_shape=results, in_specs=[hbm] * 6, out_specs=(...]
where the time goes in v4:
time: 21.5 us; the launch traced here: 21.4 us
  Pallas kernels  20.6 us (96%)
  between operations  0.8 us (4%)
    pallas_call x1, Pallas kernels, local_fn(): pl.pallas_call(kernel, out_shape=results, in_specs=[hbm] * 6, out_specs=(...  19.6 us
    pallas_call x1, Pallas kernels, local_fn(): pl.pallas_call(write_out, out_shape=results, in_specs=[vmem] * 3, out_spe...  0.99 us

profile of v4, /device:TPU:1, one launch (start us, length us, event | category | flops | bytes accessed | tf_op | source)
XLA Modules:
  0.0 21.4 jit_solution(3906709081718677269)
XLA Ops:
  0.6 19.6 %attention_backward.1 = (bf16[3072,128]{1,0:T(8,128)(2,1)S(1)}, bf16[512,128]{1,0:T(8,128)(2,1)S(1)}, bf16[512,128]{1,0:T(8,128)(2,1)S(1)}) custom-call(bf16[3072,128]{1,0:T(8,128)(2,1)} %bitcast.13, bf16[512,128]{1,0:T(8,128)(2,1)} %k_hbm.1, bf16[512,128]{1,0:T(8,128)(2,1)} %v_hbm.1, bf16[3072,128]{1,0:T(8,128)(2,1)} %bitcast.14, ...), custom_call_target="tpu_custom_call" | custom-call | tf_op jit(solution)/shard_map/attention_backward/pallas_call | solution.py:328
  20.2 1.0 %write_out.1 = (bf16[3072,128]{1,0:T(8,128)(2,1)}, bf16[512,128]{1,0:T(8,128)(2,1)}, bf16[512,128]{1,0:T(8,128)(2,1)}) custom-call(bf16[3072,128]{1,0:T(8,128)(2,1)S(1)} %get-tuple-element.9.gq_v, bf16[512,128]{1,0:T(8,128)(2,1)S(1)} %get-tuple-element.10.gk_v, bf16[512,128]{1,0:T(8,128)(2,1)S(1)} %get-tuple-element.11.gv_v), custom_call_target="tpu_custom_call" | custom-call | tf_op jit(solution)/shard_map/write_out/pallas_call | solution.py:344

commit v5 on v4

--- a/solution.py
+++ b/solution.py
@@ -23,7 +23,7 @@
 
 
 def kernel(q_hbm, k_hbm, v_hbm, o_hbm, do_hbm, lse_hbm, gq_ref, gk_ref, gv_ref,
-           x_v, lse_v, lcol, dcol, kv, acc, dq, dqr, lr, cr, pr, fr, fs, fb, ld, ss, rs, go):
+           x_v, lse_v, lcol, dcol, kv, acc, dq, dqr, lr, cr, pr, fr, fs, fb, ss, rs, go):
     dp = lax.axis_index('dp')
     me = lax.axis_index('cp')
     chip = me // 2
@@ -43,7 +43,7 @@
                 f()
 
     mine = pl.ds(me * T, T)
-    loads = [pltpu.make_async_copy(src, dst, ld.at[n]) for n, (src, dst) in enumerate((
+    loads = [pltpu.make_async_copy(src, dst, ss.at[n]) for n, (src, dst) in enumerate((
         (k_hbm, kv.at[0, mine]), (v_hbm, kv.at[1, mine]), (lse_hbm, lse_v.at[0]),
         (do_hbm, do_v.at[pl.ds(0, G * T)]), (o_hbm, o_v.at[pl.ds(0, G * T)]), (q_hbm, q_v.at[pl.ds(0, G * T)])))]
     for cp in loads:
@@ -77,19 +77,21 @@
     def kv_chunk(g):
         return kv.at[:, pl.ds(g * W, W)]
 
-    kv_pair = rcopy(0, 0, kv.at[:, even_rows], kv.at[:, even_rows], odd_dev)
-    dq_back = rcopy(1, 1, dq.at[MOVED], dqr, odd_dev)
+    kv_pair = rcopy(2, 0, kv.at[:, even_rows], kv.at[:, even_rows], odd_dev)
+    dq_back = rcopy(3, 1, dq.at[MOVED], dqr, odd_dev)
     moved = [rcopy(0, 0, lse_v.at[0], lse_v.at[1], even_dev), rcopy(1, 1, x_v.at[:, HALF], x_v.at[:, MOVED], even_dev)]
     local_back = rcopy(2, 2, acc.at[pl.ds(2 * even_dev, 2)], lr, even_dev)
-    kv_x = [rcopy((2, 3, 3, 4)[g], 2 + g, kv_chunk(g), kv_chunk(g), 3) for g in range(4)]
+    kv_x = [rcopy((0, 1, 3, 4)[g], 2 + g, kv_chunk(g), kv_chunk(g), 3) for g in range(4)]
     kv_f = [rcopy(3 + g % 2, 3 + g, kv_chunk(g), kv_chunk(g), 2) for g in range(4)]
-    first_sum = [rcopy(5 + 2 * n, 7 + 2 * n, acc.at[0, n], cr.at[0, n], 2) for n in range(2)]
-    chip_sum = [None, rcopy(6, 8, acc.at[1], cr.at[1], 2)]
-    chip_sum += [rcopy(2 + g, 4 + g, acc.at[g], cr.at[g], 3) for g in range(2, 4)]
-    part = [rcopy(5 + c, 8 + c, acc.at[2 + c], pr.at[c], 3) for c in range(2)]
-    first_back = [rcopy(2 + 4 * n, 3 + 2 * n, acc.at[0, n], fr.at[0, n], 0) for n in range(2)]
-    back = [None, rcopy(3, 4, acc.at[1], fr.at[1], 0)]
-    back += [rcopy(5 + c, 2 + c, fs.at[c], fb.at[c], 1) for c in range(2)]
+    sum0 = [rcopy(5 + n, 7 + n, acc.at[0, n], cr.at[0, n], 2) for n in range(2)]
+    sum1 = rcopy(7, 9, acc.at[1], cr.at[1], 2)
+    sum2 = rcopy(5, 6, acc.at[2], cr.at[2], 3)
+    sum3 = [rcopy(6 + n, 7 + n, acc.at[3, n], cr.at[3, n], 3) for n in range(2)]
+    part = [rcopy(5 + c, 9 + c, acc.at[2 + c], pr.at[c], 3) for c in range(2)]
+    back0 = [rcopy(n, 3 + n, acc.at[0, n], fr.at[0, n], 0) for n in range(2)]
+    back1 = rcopy(4, 5, acc.at[1], fr.at[1], 0)
+    back2 = rcopy(5, 2, fs.at[0], fb.at[0], 1)
+    back3 = [rcopy(6 + n, 3 + n, fs.at[1, n], fb.at[1, n], 1) for n in range(2)]
 
     with scope('wait_kv'):
         loads[0].wait()
@@ -184,20 +186,30 @@
     def return_chunk(g):
         if g == 0:
             for n in range(2):
-                first_sum[n].wait_recv()
+                sum0[n].wait_recv()
                 acc[0, n] += cr[0, n]
-                first_back[n].start()
-            return
-        chip_sum[g].wait_recv()
-        if g == 1:
-            acc[g] += cr[g]
+                back0[n].start()
+        elif g == 1:
+            sum1.wait_recv()
+            acc[1] += cr[1]
+            back1.start()
+        elif g == 2:
+            sum2.wait_recv()
+            part[0].wait_recv()
+            total = acc[2] + cr[2] + pr[0]
+            fs[0, 0] = (total[0] * SCALE).astype(BF16)
+            fs[0, 1] = total[1].astype(BF16)
+            sum0[0].wait_send()
+            back2.start()
         else:
-            part[g - 2].wait_recv()
-            total = acc[g] + cr[g] + pr[g - 2]
-            fs[g - 2, 0] = (total[0] * SCALE).astype(BF16)
-            fs[g - 2, 1] = total[1].astype(BF16)
-            (first_sum[0] if g == 2 else chip_sum[1]).wait_send()
-        back[g].start()
+            part[1].wait_recv()
+            sum0[1].wait_send()
+            sum1.wait_send()
+            for n in range(2):
+                sum3[n].wait_recv()
+                total = acc[3, n] + cr[3, n] + pr[1, n]
+                fs[1, n] = (total * SCALE if n == 0 else total).astype(BF16)
+                back3[n].start()
 
     with scope('diag_a'):
         diag_step((0, 2), G)
@@ -230,10 +242,10 @@
                 chunk_step(g)
             with scope('sum'):
                 if g < 2:
-                    when(odd == 1, *(cp.start for cp in (chip_sum[1:2] if g else first_sum)), lambda: forward(g + 1))
+                    when(odd == 1, *(cp.start for cp in ([sum1] if g else sum0)), lambda: forward(g + 1))
                     when(odd == 0, lambda: return_chunk(g))
                 else:
-                    when(odd == 0, chip_sum[g].start)
+                    when(odd == 0, *(cp.start for cp in ([sum2] if g == 2 else sum3)))
             if g == 1:
                 with scope('diag_b'):
                     @pl.when(odd == 1)
@@ -279,16 +291,19 @@
 
         @pl.when(me == 0)
         def _():
-            for cp in first_back + back[1:2]:
+            for cp in back0 + [back1]:
                 cp.wait_recv()
             acc[own] += fr[...]
 
         @pl.when(me == 1)
         def _():
-            for c in range(2):
-                back[2 + c].wait_recv()
-                gk_ref[c * W:(c + 1) * W, :] = jnp.transpose(fb[c, 0])
-                gv_ref[c * W:(c + 1) * W, :] = jnp.transpose(fb[c, 1])
+            back2.wait_recv()
+            gk_ref[0:W, :] = jnp.transpose(fb[0, 0])
+            gv_ref[0:W, :] = jnp.transpose(fb[0, 1])
+            back3[0].wait_recv()
+            gk_ref[W:T, :] = jnp.transpose(fb[1, 0])
+            back3[1].wait_recv()
+            gv_ref[W:T, :] = jnp.transpose(fb[1, 1])
 
         @pl.when(me != 1)
         def _():
@@ -301,8 +316,8 @@
         when(odd == 1, moved[0].wait_send, moved[1].wait_send, local_back.wait_send)
         when(me == 0, kv_x[0].wait_send, kv_x[1].wait_send)
         when(me == 1, kv_x[2].wait_send, kv_x[3].wait_send, part[0].wait_send, part[1].wait_send)
-        when(me == 2, *(cp.wait_send for cp in first_back + back[1:2] + chip_sum[2:]))
-        when(me == 3, *(cp.wait_send for cp in kv_f[2:] + first_sum[1:] + back[2:]))
+        when(me == 2, *(cp.wait_send for cp in back0 + [back1, sum2] + sum3))
+        when(me == 3, *(cp.wait_send for cp in kv_f[2:] + [back2] + back3))
 
 
 def write_out(gq_v, gk_v, gv_v, gq_hbm, gk_hbm, gv_hbm, sem):
@@ -336,7 +351,7 @@
                 pltpu.VMEM((G * T // 2, E), F32), pltpu.VMEM((2, 2, E, W), F32), pltpu.VMEM((4, 2, E, W), F32),
                 pltpu.VMEM((2, 2, E, W), F32), pltpu.VMEM((2, 2, E, W), F32),
                 pltpu.VMEM((2, 2, E, W), BF16), pltpu.VMEM((2, 2, E, W), BF16),
-                pltpu.SemaphoreType.DMA((6,)), pltpu.SemaphoreType.DMA((8,)), pltpu.SemaphoreType.DMA((10,)), pltpu.SemaphoreType.REGULAR,
+                pltpu.SemaphoreType.DMA((8,)), pltpu.SemaphoreType.DMA((11,)), pltpu.SemaphoreType.REGULAR,
             ],
             compiler_params=pltpu.CompilerParams(collective_id=0, has_side_effects=True, vmem_limit_bytes=40 * 2 ** 20),
             name='attention_backward',

time: 21.5 us -> 21.4 us (level)
  no operation moved by 1% of the time
where the time goes in v5:
time: 21.4 us; the launch traced here: 21.3 us
  Pallas kernels  20.5 us (96%)
  between operations  0.8 us (4%)
    pallas_call x1, Pallas kernels, local_fn(): pl.pallas_call(kernel, out_shape=results, in_specs=[hbm] * 6, out_specs=(...  19.5 us
    pallas_call x1, Pallas kernels, local_fn(): pl.pallas_call(write_out, out_shape=results, in_specs=[vmem] * 3, out_spe...  0.99 us

profile of v5, /device:TPU:1, one launch (start us, length us, event | category | flops | bytes accessed | tf_op | source)
XLA Modules:
  0.0 21.3 jit_solution(14323205930511298691)
XLA Ops:
  0.6 19.5 %attention_backward.1 = (bf16[3072,128]{1,0:T(8,128)(2,1)S(1)}, bf16[512,128]{1,0:T(8,128)(2,1)S(1)}, bf16[512,128]{1,0:T(8,128)(2,1)S(1)}) custom-call(bf16[3072,128]{1,0:T(8,128)(2,1)} %bitcast.13, bf16[512,128]{1,0:T(8,128)(2,1)} %k_hbm.1, bf16[512,128]{1,0:T(8,128)(2,1)} %v_hbm.1, bf16[3072,128]{1,0:T(8,128)(2,1)} %bitcast.14, ...), custom_call_target="tpu_custom_call" | custom-call | tf_op jit(solution)/shard_map/attention_backward/pallas_call | solution.py:343
  20.2 1.0 %write_out.1 = (bf16[3072,128]{1,0:T(8,128)(2,1)}, bf16[512,128]{1,0:T(8,128)(2,1)}, bf16[512,128]{1,0:T(8,128)(2,1)}) custom-call(bf16[3072,128]{1,0:T(8,128)(2,1)S(1)} %get-tuple-element.9.gq_v, bf16[512,128]{1,0:T(8,128)(2,1)S(1)} %get-tuple-element.10.gk_v, bf16[512,128]{1,0:T(8,128)(2,1)S(1)} %get-tuple-element.11.gv_v), custom_call_target="tpu_custom_call" | custom-call | tf_op jit(solution)/shard_map/write_out/pallas_call | solution.py:359

commit v6 on v5

--- a/solution.py
+++ b/solution.py
@@ -100,9 +100,14 @@
     when(me == 0, kv_x[0].start, kv_x[1].start)
 
     with scope('zero_wait_loads'):
-        acc[...] = jnp.zeros_like(acc)
-        zeros = pl.ds(4 * T, (G - 4) * T + G * T // 2)
-        dq[zeros, :] = jnp.zeros((zeros.size, E), F32)
+        @pl.loop(0, 8)
+        def _(g):
+            acc[g] = jnp.zeros((2, E, W), F32)
+
+        @pl.loop(4, G + 3)
+        def _(h):
+            dq[pl.ds(pl.multiple_of(h * T, T), T), :] = jnp.zeros((T, E), F32)
+
         for cp in loads[2:]:
             cp.wait()
 

time: 21.4 us -> 21.3 us (level)
  no operation moved by 1% of the time
where the time goes in v6:
time: 21.3 us; the launch traced here: 21.2 us
  Pallas kernels  20.5 us (96%)
  between operations  0.64 us (3%)
    pallas_call x1, Pallas kernels, local_fn(): pl.pallas_call(kernel, out_shape=results, in_specs=[hbm] * 6, out_specs=(...  19.5 us
    pallas_call x1, Pallas kernels, local_fn(): pl.pallas_call(write_out, out_shape=results, in_specs=[vmem] * 3, out_spe...  0.99 us

profile of v6, /device:TPU:1, one launch (start us, length us, event | category | flops | bytes accessed | tf_op | source)
XLA Modules:
  0.0 21.2 jit_solution(3884889935789850824)
XLA Ops:
  0.6 19.5 %attention_backward.1 = (bf16[3072,128]{1,0:T(8,128)(2,1)S(1)}, bf16[512,128]{1,0:T(8,128)(2,1)S(1)}, bf16[512,128]{1,0:T(8,128)(2,1)S(1)}) custom-call(bf16[3072,128]{1,0:T(8,128)(2,1)} %bitcast.13, bf16[512,128]{1,0:T(8,128)(2,1)} %k_hbm.1, bf16[512,128]{1,0:T(8,128)(2,1)} %v_hbm.1, bf16[3072,128]{1,0:T(8,128)(2,1)} %bitcast.14, ...), custom_call_target="tpu_custom_call" | custom-call | tf_op jit(solution)/shard_map/attention_backward/pallas_call | solution.py:348
  20.2 1.0 %write_out.1 = (bf16[3072,128]{1,0:T(8,128)(2,1)}, bf16[512,128]{1,0:T(8,128)(2,1)}, bf16[512,128]{1,0:T(8,128)(2,1)}) custom-call(bf16[3072,128]{1,0:T(8,128)(2,1)S(1)} %get-tuple-element.9.gq_v, bf16[512,128]{1,0:T(8,128)(2,1)S(1)} %get-tuple-element.10.gk_v, bf16[512,128]{1,0:T(8,128)(2,1)S(1)} %get-tuple-element.11.gv_v), custom_call_target="tpu_custom_call" | custom-call | tf_op jit(solution)/shard_map/write_out/pallas_call | solution.py:364

commit v7 on v6

--- a/solution.py
+++ b/solution.py
@@ -87,7 +87,8 @@
     sum1 = rcopy(7, 9, acc.at[1], cr.at[1], 2)
     sum2 = rcopy(5, 6, acc.at[2], cr.at[2], 3)
     sum3 = [rcopy(6 + n, 7 + n, acc.at[3, n], cr.at[3, n], 3) for n in range(2)]
-    part = [rcopy(5 + c, 9 + c, acc.at[2 + c], pr.at[c], 3) for c in range(2)]
+    part = [rcopy(5, 9, acc.at[2], pr.at[0], 3)]
+    part += [rcopy(6 + n, 10 + n, acc.at[3, n], pr.at[1, n], 3) for n in range(2)]
     back0 = [rcopy(n, 3 + n, acc.at[0, n], fr.at[0, n], 0) for n in range(2)]
     back1 = rcopy(4, 5, acc.at[1], fr.at[1], 0)
     back2 = rcopy(5, 2, fs.at[0], fb.at[0], 1)
@@ -129,12 +130,20 @@
     def chunk_step(g):
         cols = pl.ds(g * W, W)
         k, v = kv[0, cols, :], kv[1, cols, :]
-        blocks = [pl.ds(h * T, 2 * T) for h in range(0, G, 2)]
+        size = 1 if g == 0 else 2
+        blocks = [pl.ds(h * T, size * T) for h in range(0, G, size)]
         done = [scores(q_v[rows, :], do_v[rows, :], k, v, lcol[rows, :], dcol[rows, :]) for rows in blocks]
         for rows, (p, ds) in zip(blocks, done):
-            dq[rows, :] += dot(ds, k, 1, 0)
+            if g > 0:
+                dq[rows, :] += dot(ds, k, 1, 0)
             acc[g, 0] += dot(q_v[rows, :], ds, 0, 0)
             acc[g, 1] += dot(do_v[rows, :], p, 0, 0)
+
+        def rest():
+            for rows, (_, ds) in zip(blocks, done):
+                dq[rows, :] += dot(ds, k, 1, 0)
+
+        return rest
 
     def pair_step(heads):
         row0 = (1 - odd) * (G * T)
@@ -188,13 +197,13 @@
         for h in range(max(heads) + 2, setup_heads):
             rows_setup(lse_t, h, pl.ds(h * T, T))
 
+    def return_first(n):
+        sum0[n].wait_recv()
+        acc[0, n] += cr[0, n]
+        back0[n].start()
+
     def return_chunk(g):
-        if g == 0:
-            for n in range(2):
-                sum0[n].wait_recv()
-                acc[0, n] += cr[0, n]
-                back0[n].start()
-        elif g == 1:
+        if g == 1:
             sum1.wait_recv()
             acc[1] += cr[1]
             back1.start()
@@ -207,11 +216,11 @@
             sum0[0].wait_send()
             back2.start()
         else:
-            part[1].wait_recv()
             sum0[1].wait_send()
             sum1.wait_send()
             for n in range(2):
                 sum3[n].wait_recv()
+                part[1 + n].wait_recv()
                 total = acc[3, n] + cr[3, n] + pr[1, n]
                 fs[1, n] = (total * SCALE if n == 0 else total).astype(BF16)
                 back3[n].start()
@@ -228,7 +237,7 @@
     with scope('diag_b'):
         when(me != 3, lambda: diag_step((4,), 0))
 
-    when(me == 1, kv_x[2].start, kv_x[3].start, part[0].start, part[1].start)
+    when(me == 1, kv_x[2].start, kv_x[3].start, *(cp.start for cp in part))
 
     def forward(g):
         kv_x[g].wait_recv()
@@ -244,11 +253,17 @@
             with scope('wait_f'):
                 when(odd == 0, kv_f[g].wait_recv)
             with scope('cross'):
-                chunk_step(g)
+                rest = chunk_step(g)
             with scope('sum'):
                 if g < 2:
-                    when(odd == 1, *(cp.start for cp in ([sum1] if g else sum0)), lambda: forward(g + 1))
-                    when(odd == 0, lambda: return_chunk(g))
+                    when(odd == 1, *(cp.start for cp in ([sum1] if g else sum0)))
+                    if g == 0:
+                        when(odd == 0, lambda: return_first(0))
+                        rest()
+                        when(odd == 0, lambda: return_first(1))
+                    else:
+                        when(odd == 0, lambda: return_chunk(1))
+                    when(odd == 1, lambda: forward(g + 1))
                 else:
                     when(odd == 0, *(cp.start for cp in ([sum2] if g == 2 else sum3)))
             if g == 1:
@@ -320,7 +335,7 @@
         when(odd == 0, kv_pair.wait_send, dq_back.wait_send)
         when(odd == 1, moved[0].wait_send, moved[1].wait_send, local_back.wait_send)
         when(me == 0, kv_x[0].wait_send, kv_x[1].wait_send)
-        when(me == 1, kv_x[2].wait_send, kv_x[3].wait_send, part[0].wait_send, part[1].wait_send)
+        when(me == 1, kv_x[2].wait_send, kv_x[3].wait_send, *(cp.wait_send for cp in part))
         when(me == 2, *(cp.wait_send for cp in back0 + [back1, sum2] + sum3))
         when(me == 3, *(cp.wait_send for cp in kv_f[2:] + [back2] + back3))
 
@@ -356,7 +371,7 @@
                 pltpu.VMEM((G * T // 2, E), F32), pltpu.VMEM((2, 2, E, W), F32), pltpu.VMEM((4, 2, E, W), F32),
                 pltpu.VMEM((2, 2, E, W), F32), pltpu.VMEM((2, 2, E, W), F32),
                 pltpu.VMEM((2, 2, E, W), BF16), pltpu.VMEM((2, 2, E, W), BF16),
-                pltpu.SemaphoreType.DMA((8,)), pltpu.SemaphoreType.DMA((11,)), pltpu.SemaphoreType.REGULAR,
+                pltpu.SemaphoreType.DMA((8,)), pltpu.SemaphoreType.DMA((12,)), pltpu.SemaphoreType.REGULAR,
             ],
             compiler_params=pltpu.CompilerParams(collective_id=0, has_side_effects=True, vmem_limit_bytes=40 * 2 ** 20),
             name='attention_backward',

time: 21.3 us -> 21.3 us (level)
  no operation moved by 1% of the time
where the time goes in v7:
time: 21.3 us; the launch traced here: 21.2 us
  Pallas kernels  20.5 us (96%)
  between operations  0.64 us (3%)
    pallas_call x1, Pallas kernels, local_fn(): pl.pallas_call(kernel, out_shape=results, in_specs=[hbm] * 6, out_specs=(...  19.6 us
    pallas_call x1, Pallas kernels, local_fn(): pl.pallas_call(write_out, out_shape=results, in_specs=[vmem] * 3, out_spe...  0.99 us

profile of v7, /device:TPU:1, one launch (start us, length us, event | category | flops | bytes accessed | tf_op | source)
XLA Modules:
  0.0 21.2 jit_solution(11327728458030722138)
XLA Ops:
  0.6 19.6 %attention_backward.1 = (bf16[3072,128]{1,0:T(8,128)(2,1)S(1)}, bf16[512,128]{1,0:T(8,128)(2,1)S(1)}, bf16[512,128]{1,0:T(8,128)(2,1)S(1)}) custom-call(bf16[3072,128]{1,0:T(8,128)(2,1)} %bitcast.13, bf16[512,128]{1,0:T(8,128)(2,1)} %k_hbm.1, bf16[512,128]{1,0:T(8,128)(2,1)} %v_hbm.1, bf16[3072,128]{1,0:T(8,128)(2,1)} %bitcast.14, ...), custom_call_target="tpu_custom_call" | custom-call | tf_op jit(solution)/shard_map/attention_backward/pallas_call | solution.py:363
  20.2 1.0 %write_out.1 = (bf16[3072,128]{1,0:T(8,128)(2,1)}, bf16[512,128]{1,0:T(8,128)(2,1)}, bf16[512,128]{1,0:T(8,128)(2,1)}) custom-call(bf16[3072,128]{1,0:T(8,128)(2,1)S(1)} %get-tuple-element.9.gq_v, bf16[512,128]{1,0:T(8,128)(2,1)S(1)} %get-tuple-element.10.gk_v, bf16[512,128]{1,0:T(8,128)(2,1)S(1)} %get-tuple-element.11.gv_v), custom_call_target="tpu_custom_call" | custom-call | tf_op jit(solution)/shard_map/write_out/pallas_call | solution.py:379
